TPU v7x, 32 devices: a whole 2x2x4 slice. The times are simulated.
32 devices in a mesh: fsdp: 8 (over y, x, core), model: 4 (over z).
Axes of the slice: x: 2, y: 2, z: 4, core: 2. Of those that a mesh axis runs over, the one named last changes fastest.
Arguments:
- w_query: float32 [4096, 4096], P('fsdp', 'model'), may hold values from -0.125 to 0.125
- first_query: float32 [4096, 4096], P('fsdp', 'model'), may hold values from -0.09375 to 0.09375
- second_query: float32 [4096, 4096], P('fsdp', 'model'), may hold values from -0.09375 to 0.09375
- w_key: float32 [4096, 4096], P('fsdp', 'model'), may hold values from -0.125 to 0.125
- first_key: float32 [4096, 4096], P('fsdp', 'model'), may hold values from -0.09375 to 0.09375
- second_key: float32 [4096, 4096], P('fsdp', 'model'), may hold values from -0.09375 to 0.09375
- w_value: float32 [4096, 4096], P('fsdp', 'model'), may hold values from -0.125 to 0.125
- first_value: float32 [4096, 4096], P('fsdp', 'model'), may hold values from -0.09375 to 0.09375
- second_value: float32 [4096, 4096], P('fsdp', 'model'), may hold values from -0.09375 to 0.09375
- norm_gain: float32 [4096], P('fsdp'), may hold values from 0.25 to 1.75
Outputs:
- ready_query: bfloat16 [4096, 4096], P(None, 'model')
- ready_key: bfloat16 [4096, 4096], P(None, 'model')
- ready_value: bfloat16 [4096, 4096], P(None, 'model')
- factor_query: float32 [4096], P('model')
- factor_key: float32 [4096], P('model')
- factor_value: float32 [4096], P('model')
All inputs are finite; a program needn't handle non-finite values. Where the computation divides by a largest or mean magnitude, that divisor is 1e-20 or more.
Results may differ from a plain program's by a relative error of at most 0.001.
Values may be sent and summed in bfloat16 or wider, within the bound.
A program may use at most 128 MiB of HBM per device.

v0:
```python
import functools
import math

import jax
import jax.numpy as jnp
from jax import lax
from jax.experimental import pallas as pl
from jax.experimental.pallas import tpu as pltpu
from jax.sharding import PartitionSpec as P

learn_rate = 0.2
hold_rate = 0.9
MESH = pl.DeviceIdType.MESH
UNITS = 4
PARTS = ((1, 1, 2), (2, 2), (2, 1, 1))
STEP = 32
AHEAD = 2
VMEM_BYTES = 67_043_328


def plain(
    w_query,
    first_query,
    second_query,
    w_key,
    first_key,
    second_key,
    w_value,
    first_value,
    second_value,
    norm_gain,
    rows,
):
    gained = []
    for w, first, second in (
        (w_query, first_query, second_query),
        (w_key, first_key, second_key),
        (w_value, first_value, second_value),
    ):
        hold = hold_rate * first + second
        gained.append((w - learn_rate * hold) * norm_gain[:, None])
    totals = lax.psum(tuple(jnp.sum(jnp.abs(g), axis=0) for g in gained), "fsdp")
    factors = tuple(t / rows for t in totals)
    ready = tuple(
        lax.all_gather(
            (g / f).astype(jnp.bfloat16), "fsdp", axis=0, tiled=True
        )
        for g, f in zip(gained, factors)
    )
    return ready + factors


def units_of(cols):
    units = []
    for m, sizes in enumerate(PARTS):
        first = 0
        for size in sizes:
            units.append((m, first, size * cols // UNITS))
            first += size * cols // UNITS
    return units


def gather_kernel(total_rows, *refs):
    ins, gain_ref = refs[:9], refs[9]
    outs, factor_ref = refs[10:13], refs[13]
    (
        w_buf, first_buf, second_buf, gain_line, gain_buf, mine, parts,
        load_sem, gain_sem, sum_send, sum_recv, x_recv, y_recv, diag_recv,
        chip_recv, send_sem,
    ) = refs[14:]
    bufs = (w_buf, first_buf, second_buf)
    rows, cols = w_buf.shape[1:]
    half = rows // 2

    me = lax.axis_index("fsdp")
    core = me % 2
    x = (me // 2) % 2
    y = me // 4
    partner = me + 1 - 2 * core
    x_near = me + 2 - 4 * x
    y_near = me + 4 - 8 * y
    diag = x_near + 4 - 8 * y
    peers = [
        partner, x_near, y_near, diag,
        x_near + 1 - 2 * core, y_near + 1 - 2 * core, diag + 1 - 2 * core,
    ]

    units = units_of(cols)
    loads = []
    for u, (m, c, width) in enumerate(units):
        at = pl.ds(c, width)
        loads.append([
            pltpu.make_async_copy(
                ins[3 * m + k].at[:, at], bufs[k].at[m, :, at], load_sem.at[u, k]
            )
            for k in range(3)
        ])

    def load(u):
        if u < len(units):
            for copy in loads[u]:
                copy.start()

    gain_copy = pltpu.make_async_copy(gain_ref, gain_line, gain_sem)
    gain_copy.start()
    for u in range(AHEAD):
        load(u)

    barrier = pltpu.get_barrier_semaphore()
    for peer in peers:
        pl.semaphore_signal(
            barrier, inc=1, device_id={"fsdp": peer}, device_id_type=MESH
        )

    gain_copy.wait()
    for k in range(rows // 128):
        line = gain_line[:, pl.ds(k * 128, 128)]
        gain_buf[pl.ds(k * 128, 128), :] = jnp.broadcast_to(line, (128, 128)).T

    def sums(u):
        m, c, width = units[u]
        for copy in loads[u]:
            copy.wait()
        load(u + AHEAD)
        tiles = width // 128

        def body(i, acc):
            at = pl.ds(pl.multiple_of(i * STEP, STEP), STEP)
            gain = gain_buf[at, :]
            new = []
            for t in range(tiles):
                lanes = pl.ds(c + t * 128, 128)
                hold = hold_rate * first_buf[m, at, lanes] + second_buf[m, at, lanes]
                gained = (w_buf[m, at, lanes] - learn_rate * hold) * gain
                w_buf[m, at, lanes] = gained
                size = jnp.abs(gained)
                new.append(
                    acc[t] + jnp.sum(size.reshape(STEP // 8, 8, 128), axis=0)
                )
            return tuple(new)

        acc = lax.fori_loop(
            0, rows // STEP, body,
            tuple(jnp.zeros((8, 128), jnp.float32) for _ in range(tiles)),
        )
        for t in range(tiles):
            mine[u, :, pl.ds(t * 128, 128)] = jnp.sum(acc[t], axis=0, keepdims=True)

    def sum_copy(u, slot, peer):
        return pltpu.make_async_remote_copy(
            src_ref=mine.at[u, :, pl.ds(0, units[u][2])],
            dst_ref=parts.at[u, slot, :, pl.ds(0, units[u][2])],
            send_sem=sum_send.at[u, slot],
            recv_sem=sum_recv.at[u, slot],
            device_id={"fsdp": peer},
            device_id_type=MESH,
        )

    def send_sums(u):
        for slot, peer in enumerate(peers):
            sum_copy(u, slot, peer).start()

    def block(u, owner, first, count):
        m, c, width = units[u]
        at = pl.ds(pl.multiple_of(owner * rows + first, 16), count)
        return outs[m].at[at, pl.ds(c, width)]

    def send(m, ref, recv_sem, peer):
        pltpu.make_async_remote_copy(
            src_ref=ref, dst_ref=ref, send_sem=send_sem.at[m], recv_sem=recv_sem,
            device_id={"fsdp": peer}, device_id_type=MESH,
        ).start()

    def arrived(ref, recv_sem):
        pltpu.make_async_remote_copy(
            src_ref=ref, dst_ref=ref, send_sem=send_sem.at[0], recv_sem=recv_sem,
            device_id={"fsdp": partner}, device_id_type=MESH,
        ).wait_recv()

    def finish(u):
        m, c, width = units[u]
        for slot, peer in enumerate(peers):
            sum_copy(u, slot, peer).wait_recv()
        total = mine[u, :, pl.ds(0, width)]
        for slot in range(7):
            total = total + parts[u, slot, :, pl.ds(0, width)]
        factor = total / total_rows
        factor_ref[pl.ds(m, 1), pl.ds(c, width)] = factor
        scale = jnp.broadcast_to(1.0 / factor, (16, width))

        def body(i, carry):
            for k in range(STEP // 16):
                at = pl.multiple_of(i * STEP + k * 16, 16)
                tile = w_buf[m, pl.ds(at, 16), pl.ds(c, width)] * scale
                outs[m][
                    pl.ds(pl.multiple_of(me * rows + at, 16), 16),
                    pl.ds(c, width),
                ] = tile.astype(jnp.bfloat16)
            return carry

        for h in range(2):
            lo = h * half // STEP
            lax.fori_loop(lo, lo + half // STEP, body, 0)
            ref = block(u, me, h * half, half)
            send(m, ref, x_recv.at[u, h], x_near)
            send(m, ref, y_recv.at[u, h], y_near)
        send(m, block(u, me, 0, rows), chip_recv.at[m], partner)

    count = len(units)
    for u in range(count):
        sums(u)
        if u == 0:
            pl.semaphore_wait(barrier, 7)
        send_sums(u)
        if u >= 1:
            finish(u - 1)
    finish(count - 1)

    for u, (m, _, _) in enumerate(units):
        for h in range(2):
            ref = block(u, x_near, h * half, half)
            arrived(ref, x_recv.at[u, h])
            if h == 0:
                send(m, ref, diag_recv.at[u, 0], y_near)
            send(m, ref, chip_recv.at[m], partner)
            ref = block(u, y_near, h * half, half)
            arrived(ref, y_recv.at[u, h])
            if h == 1:
                send(m, ref, diag_recv.at[u, 1], x_near)
            send(m, ref, chip_recv.at[m], partner)
    for u, (m, _, _) in enumerate(units):
        for h in range(2):
            ref = block(u, diag, h * half, half)
            arrived(ref, diag_recv.at[u, h])
            send(m, ref, chip_recv.at[m], partner)

    for m in range(3):
        taken = outs[m].at[pl.ds(0, 4 * rows), :]
        sent = outs[m].at[pl.ds(0, 7 * rows), :]
        arrived(taken, chip_recv.at[m])
        pltpu.make_async_remote_copy(
            src_ref=sent, dst_ref=sent, send_sem=send_sem.at[m],
            recv_sem=chip_recv.at[m], device_id={"fsdp": partner},
            device_id_type=MESH,
        ).wait_send()
    for u in range(count):
        for slot, peer in enumerate(peers):
            sum_copy(u, slot, peer).wait_send()


def write_kernel(a, b, c, factor, out_a, out_b, out_c, fa, fb, fc, sem):
    copies = []
    for k, (src, dst) in enumerate(((a, out_a), (b, out_b), (c, out_c))):
        rows = src.shape[0] // 4
        for p in range(4):
            at = pl.ds(p * rows, rows)
            copies.append(
                pltpu.make_async_copy(src.at[at, :], dst.at[at, :], sem.at[k, p])
            )
    for copy in copies:
        copy.start()
    for m, out in enumerate((fa, fb, fc)):
        out[...] = factor[m, :]
    for copy in copies:
        copy.wait()


def ringed(*args, total_rows):
    rows, cols = args[0].shape
    units = units_of(cols)
    count = len(units)
    width = max(unit[2] for unit in units)
    big = (8 * rows, cols)
    vmem = pl.BlockSpec(memory_space=pltpu.VMEM)
    hbm = pl.BlockSpec(memory_space=pltpu.HBM)
    buf = pltpu.VMEM((3, rows, cols), jnp.float32)
    dma = pltpu.SemaphoreType.DMA
    *gathered, factor = pl.pallas_call(
        functools.partial(gather_kernel, total_rows),
        out_shape=[pltpu.VMEM(big, jnp.bfloat16)] * 3
        + [pltpu.VMEM((3, cols), jnp.float32)],
        in_specs=[hbm] * 10,
        out_specs=[vmem] * 4,
        scratch_shapes=[
            buf, buf, buf,
            pltpu.VMEM((1, rows), jnp.float32),
            pltpu.VMEM((rows, 128), jnp.float32),
            pltpu.VMEM((count, 1, width), jnp.float32),
            pltpu.VMEM((count, 7, 1, width), jnp.float32),
            dma((count, 3)), dma,
            dma((count, 7)), dma((count, 7)),
            dma((count, 2)), dma((count, 2)), dma((count, 2)),
            dma((3,)), dma((3,)),
        ],
        compiler_params=pltpu.CompilerParams(
            collective_id=0, has_side_effects=True,
            vmem_limit_bytes=VMEM_BYTES - 3 * 16 * rows * cols - 2**20,
        ),
        name="gather",
    )(*(
        pltpu.with_memory_space_constraint(a, pltpu.HBM)
        for a in (*args[:9], args[9].reshape(1, rows))
    ))
    ready = jax.ShapeDtypeStruct(big, jnp.bfloat16)
    line = jax.ShapeDtypeStruct((cols,), jnp.float32)
    return pl.pallas_call(
        write_kernel,
        out_shape=[ready] * 3 + [line] * 3,
        in_specs=[vmem] * 4,
        out_specs=[hbm] * 3 + [vmem] * 3,
        scratch_shapes=[dma((3, 4))],
        compiler_params=pltpu.CompilerParams(vmem_limit_bytes=2**20),
        name="write",
    )(*gathered, factor)


def on_device(*args, devices):
    rows, cols = args[0].shape
    total_rows = devices * rows
    fits = rows * cols * (36 + 48) <= 48 * 2**20
    if devices == 8 and rows % 128 == 0 and cols % (128 * UNITS) == 0 and fits:
        return tuple(ringed(*args, total_rows=total_rows))
    return plain(*args, rows=total_rows)


def solution(mesh):
    return jax.shard_map(
        functools.partial(on_device, devices=mesh.shape["fsdp"]),
        mesh=mesh,
        in_specs=(P("fsdp", "model"),) * 9 + (P("fsdp"),),
        out_specs=(P(None, "model"),) * 3 + (P("model"),) * 3,
        check_vma=False,
    )
```

profile of v0, /device:TPU:0, one launch (start us, length us, event | category | flops | bytes accessed | tf_op | source)
XLA Modules:
  0.0 123.7 jit_solution(394601932589446835)
XLA Ops:
  0.6 114.0 %gather.1 = (bf16[4096,1024]{1,0:T(8,128)(2,1)S(1)}, bf16[4096,1024]{1,0:T(8,128)(2,1)S(1)}, bf16[4096,1024]{1,0:T(8,128)(2,1)S(1)}, f32[3,1024]{1,0:T(4,128)S(1)}) custom-call(f32[512,1024]{1,0:T(8,128)} %refs_0_.1, f32[512,1024]{1,0:T(8,128)} %refs_1_.1, f32[512,1024]{1,0:T(8,128)} %refs_2_.1, f32[512,1024]{1,0:T(8,128)} %refs_3_.1, f32[512,1024]{1,0:T(8,128)} %refs_4_.1, ...), custom_call_target="tpu_custom_call" | custom-call | tf_op jit(solution)/shard_map/gather/pallas_call | solution.py:278
  114.6 9.1 %write.1 = (bf16[4096,1024]{1,0:T(8,128)(2,1)}, bf16[4096,1024]{1,0:T(8,128)(2,1)}, bf16[4096,1024]{1,0:T(8,128)(2,1)}, f32[1024]{0:T(1024)}, f32[1024]{0:T(1024)}, /*index=5*/f32[1024]{0:T(1024)}) custom-call(bf16[4096,1024]{1,0:T(8,128)(2,1)S(1)} %get-tuple-element.10.a, bf16[4096,1024]{1,0:T(8,128)(2,1)S(1)} %get-tuple-element.11.b, ...), custom_call_target="tpu_custom_call" | custom-call | tf_op jit(solution)/shard_map/write/pallas_call | solution.py:306
where the time goes:
time: 124 us
  Pallas kernels  123 us (99%)
    pallas_call x1, Pallas kernels, ringed(): pl.pallas_call(functools.partial(gather_kernel, total_rows), out_shape=[p...  114 us
    pallas_call x1, Pallas kernels, ringed(): pl.pallas_call(write_kernel, out_shape=[ready] * 3 + [line] * 3, in_specs...  9.08 us

commit v1 on v0

--- a/solution.py
+++ b/solution.py
@@ -11,10 +11,11 @@
 learn_rate = 0.2
 hold_rate = 0.9
 MESH = pl.DeviceIdType.MESH
-UNITS = 4
-PARTS = ((1, 1, 2), (2, 2), (2, 1, 1))
+UNITS = 8
+PARTS = ((1, 2, 5), (8,), (4, 2, 1, 1))
 STEP = 32
-AHEAD = 2
+START = 1
+AHEAD = 3
 VMEM_BYTES = 67_043_328
 
 
@@ -60,16 +61,23 @@
     return units
 
 
+def diag_slot(units, u):
+    m = units[u][0]
+    if m < 2:
+        return m
+    return 2 + sum(unit[0] == 2 for unit in units[:u])
+
+
 def gather_kernel(total_rows, *refs):
     ins, gain_ref = refs[:9], refs[9]
     outs, factor_ref = refs[10:13], refs[13]
     (
-        w_buf, first_buf, second_buf, gain_line, gain_buf, mine, parts,
-        load_sem, gain_sem, sum_send, sum_recv, x_recv, y_recv, diag_recv,
-        chip_recv, send_sem,
+        bufs, gain_line, gain_buf, mine, parts, early,
+        load_sem, gain_sem, sum_send, sum_recv, early_send, early_recv,
+        x_recv, y_recv, x_rest, y_rest, diag_recv, chip_recv, send_sem,
     ) = refs[14:]
-    bufs = (w_buf, first_buf, second_buf)
-    rows, cols = w_buf.shape[1:]
+    w_buf, first_buf, second_buf = (bufs.at[k] for k in range(3))
+    rows, cols = bufs.shape[2:]
     half = rows // 2
 
     me = lax.axis_index("fsdp")
@@ -84,27 +92,9 @@
         partner, x_near, y_near, diag,
         x_near + 1 - 2 * core, y_near + 1 - 2 * core, diag + 1 - 2 * core,
     ]
-
     units = units_of(cols)
-    loads = []
-    for u, (m, c, width) in enumerate(units):
-        at = pl.ds(c, width)
-        loads.append([
-            pltpu.make_async_copy(
-                ins[3 * m + k].at[:, at], bufs[k].at[m, :, at], load_sem.at[u, k]
-            )
-            for k in range(3)
-        ])
-
-    def load(u):
-        if u < len(units):
-            for copy in loads[u]:
-                copy.start()
-
-    gain_copy = pltpu.make_async_copy(gain_ref, gain_line, gain_sem)
-    gain_copy.start()
-    for u in range(AHEAD):
-        load(u)
+    count = len(units)
+    early_width = units[0][2]
 
     barrier = pltpu.get_barrier_semaphore()
     for peer in peers:
@@ -112,6 +102,26 @@
             barrier, inc=1, device_id={"fsdp": peer}, device_id_type=MESH
         )
 
+    def load(u):
+        if u < count:
+            m, c, width = units[u]
+            at = pl.ds(c, width)
+            for k in range(3):
+                pltpu.make_async_copy(
+                    ins[3 * m + k].at[:, at], bufs.at[k, m, :, at],
+                    load_sem.at[u % 4],
+                ).start()
+
+    def loaded(u):
+        m, c, width = units[u]
+        ref = bufs.at[:, m, :, pl.ds(c, width)]
+        pltpu.make_async_copy(ref, ref, load_sem.at[u % 4]).wait()
+
+    gain_copy = pltpu.make_async_copy(gain_ref, gain_line, gain_sem)
+    gain_copy.start()
+    for u in range(START):
+        load(u)
+
     gain_copy.wait()
     for k in range(rows // 128):
         line = gain_line[:, pl.ds(k * 128, 128)]
@@ -119,8 +129,10 @@
 
     def sums(u):
         m, c, width = units[u]
-        for copy in loads[u]:
-            copy.wait()
+        loaded(u)
+        if u == 0:
+            for v in range(START, AHEAD):
+                load(v)
         load(u + AHEAD)
         tiles = width // 128
 
@@ -144,25 +156,22 @@
             tuple(jnp.zeros((8, 128), jnp.float32) for _ in range(tiles)),
         )
         for t in range(tiles):
-            mine[u, :, pl.ds(t * 128, 128)] = jnp.sum(acc[t], axis=0, keepdims=True)
-
-    def sum_copy(u, slot, peer):
-        return pltpu.make_async_remote_copy(
-            src_ref=mine.at[u, :, pl.ds(0, units[u][2])],
-            dst_ref=parts.at[u, slot, :, pl.ds(0, units[u][2])],
-            send_sem=sum_send.at[u, slot],
-            recv_sem=sum_recv.at[u, slot],
-            device_id={"fsdp": peer},
-            device_id_type=MESH,
-        )
+            mine[m, :, pl.ds(c + t * 128, 128)] = jnp.sum(
+                acc[t], axis=0, keepdims=True
+            )
 
     def send_sums(u):
+        m, c, width = units[u]
+        at = pl.ds(c, width)
         for slot, peer in enumerate(peers):
-            sum_copy(u, slot, peer).start()
-
-    def block(u, owner, first, count):
-        m, c, width = units[u]
-        at = pl.ds(pl.multiple_of(owner * rows + first, 16), count)
+            pltpu.make_async_remote_copy(
+                src_ref=mine.at[m, :, at], dst_ref=parts.at[slot, m, :, at],
+                send_sem=sum_send, recv_sem=sum_recv.at[u],
+                device_id={"fsdp": peer}, device_id_type=MESH,
+            ).start()
+
+    def block(m, owner, first, tall, c, width):
+        at = pl.ds(pl.multiple_of(owner * rows + first, 16), tall)
         return outs[m].at[at, pl.ds(c, width)]
 
     def send(m, ref, recv_sem, peer):
@@ -177,75 +186,113 @@
             device_id={"fsdp": partner}, device_id_type=MESH,
         ).wait_recv()
 
-    def finish(u):
-        m, c, width = units[u]
-        for slot, peer in enumerate(peers):
-            sum_copy(u, slot, peer).wait_recv()
-        total = mine[u, :, pl.ds(0, width)]
-        for slot in range(7):
-            total = total + parts[u, slot, :, pl.ds(0, width)]
-        factor = total / total_rows
-        factor_ref[pl.ds(m, 1), pl.ds(c, width)] = factor
-        scale = jnp.broadcast_to(1.0 / factor, (16, width))
+    def early_copy(side, peer):
+        return pltpu.make_async_remote_copy(
+            src_ref=w_buf.at[0, pl.ds(0, half), pl.ds(0, early_width)],
+            dst_ref=early.at[side], send_sem=early_send,
+            recv_sem=early_recv.at[side],
+            device_id={"fsdp": peer}, device_id_type=MESH,
+        )
+
+    def scaled(source, m, owner, lo, hi, c, width):
+        scale = jnp.broadcast_to(
+            1.0 / factor_ref[pl.ds(m, 1), pl.ds(c, width)], (16, width)
+        )
 
         def body(i, carry):
             for k in range(STEP // 16):
                 at = pl.multiple_of(i * STEP + k * 16, 16)
-                tile = w_buf[m, pl.ds(at, 16), pl.ds(c, width)] * scale
+                tile = source[pl.ds(at, 16), pl.ds(c, width)] * scale
                 outs[m][
-                    pl.ds(pl.multiple_of(me * rows + at, 16), 16),
+                    pl.ds(pl.multiple_of(owner * rows + at, 16), 16),
                     pl.ds(c, width),
                 ] = tile.astype(jnp.bfloat16)
             return carry
 
+        lax.fori_loop(lo // STEP, hi // STEP, body, 0)
+
+    def finish(u):
+        m, c, width = units[u]
+        at = pl.ds(c, width)
+        arrived(parts.at[:, m, :, at], sum_recv.at[u])
+        total = mine[m, :, at]
+        for slot in range(7):
+            total = total + parts[slot, m, :, at]
+        factor_ref[pl.ds(m, 1), at] = total / total_rows
+        for h in (1, 0):
+            scaled(w_buf.at[m], m, me, h * half, (h + 1) * half, c, width)
+            if u == 0 and h == 0:
+                continue
+            ref = block(m, me, h * half, half, c, width)
+            send(m, ref, x_recv.at[u] if h == 0 else x_rest.at[m], x_near)
+            send(m, ref, y_recv.at[u] if h == 1 else y_rest.at[m], y_near)
+        send(m, block(m, me, 0, rows, c, width), chip_recv.at[m], partner)
+
+    def take_early():
+        for side, owner in enumerate((x_near, y_near)):
+            arrived(early.at[side], early_recv.at[side])
+            scaled(early.at[side], 0, owner, 0, half, 0, early_width)
+
+    sums(0)
+    pl.semaphore_wait(barrier, 7)
+    send_sums(0)
+    sums(1)
+    send_sums(1)
+    early_copy(0, x_near).start()
+    early_copy(1, y_near).start()
+    for u in range(2, count + 2):
+        if u < count:
+            sums(u)
+            send_sums(u)
+        finish(u - 2)
+        if u == 3:
+            take_early()
+
+    for u, (m, c, width) in enumerate(units):
+        ref = block(m, x_near, 0, half, c, width)
+        if u > 0:
+            arrived(ref, x_recv.at[u])
+        send(m, ref, diag_recv.at[0, diag_slot(units, u)], y_near)
+        send(m, ref, chip_recv.at[m], partner)
+        ref = block(m, y_near, half, half, c, width)
+        arrived(ref, y_recv.at[u])
+        send(m, ref, diag_recv.at[1, diag_slot(units, u)], x_near)
+        send(m, ref, chip_recv.at[m], partner)
+        if c + width == cols:
+            ref = block(m, x_near, half, half, 0, cols)
+            arrived(ref, x_rest.at[m])
+            send(m, ref, chip_recv.at[m], partner)
+            skip = early_width if m == 0 else 0
+            arrived(
+                block(m, y_near, 0, half, skip, cols - skip), y_rest.at[m]
+            )
+            ref = block(m, y_near, 0, half, 0, cols)
+            send(m, ref, chip_recv.at[m], partner)
+    for u, (m, c, width) in enumerate(units):
+        if m < 2:
+            if c + width < cols:
+                continue
+            c, width = 0, cols
         for h in range(2):
-            lo = h * half // STEP
-            lax.fori_loop(lo, lo + half // STEP, body, 0)
-            ref = block(u, me, h * half, half)
-            send(m, ref, x_recv.at[u, h], x_near)
-            send(m, ref, y_recv.at[u, h], y_near)
-        send(m, block(u, me, 0, rows), chip_recv.at[m], partner)
-
-    count = len(units)
-    for u in range(count):
-        sums(u)
-        if u == 0:
-            pl.semaphore_wait(barrier, 7)
-        send_sums(u)
-        if u >= 1:
-            finish(u - 1)
-    finish(count - 1)
-
-    for u, (m, _, _) in enumerate(units):
-        for h in range(2):
-            ref = block(u, x_near, h * half, half)
-            arrived(ref, x_recv.at[u, h])
-            if h == 0:
-                send(m, ref, diag_recv.at[u, 0], y_near)
-            send(m, ref, chip_recv.at[m], partner)
-            ref = block(u, y_near, h * half, half)
-            arrived(ref, y_recv.at[u, h])
-            if h == 1:
-                send(m, ref, diag_recv.at[u, 1], x_near)
-            send(m, ref, chip_recv.at[m], partner)
-    for u, (m, _, _) in enumerate(units):
-        for h in range(2):
-            ref = block(u, diag, h * half, half)
-            arrived(ref, diag_recv.at[u, h])
+            ref = block(m, diag, h * half, half, c, width)
+            arrived(ref, diag_recv.at[h, diag_slot(units, u)])
             send(m, ref, chip_recv.at[m], partner)
 
     for m in range(3):
         taken = outs[m].at[pl.ds(0, 4 * rows), :]
-        sent = outs[m].at[pl.ds(0, 7 * rows), :]
+        early_rows = rows * early_width // cols if m == 0 else 0
+        sent = outs[m].at[pl.ds(0, 7 * rows - early_rows), :]
         arrived(taken, chip_recv.at[m])
         pltpu.make_async_remote_copy(
             src_ref=sent, dst_ref=sent, send_sem=send_sem.at[m],
             recv_sem=chip_recv.at[m], device_id={"fsdp": partner},
             device_id_type=MESH,
         ).wait_send()
-    for u in range(count):
-        for slot, peer in enumerate(peers):
-            sum_copy(u, slot, peer).wait_send()
+    for ref, sem in ((parts, sum_send), (early, early_send)):
+        pltpu.make_async_remote_copy(
+            src_ref=ref, dst_ref=ref, send_sem=sem, recv_sem=sum_recv.at[0],
+            device_id={"fsdp": partner}, device_id_type=MESH,
+        ).wait_send()
 
 
 def write_kernel(a, b, c, factor, out_a, out_b, out_c, fa, fb, fc, sem):
@@ -269,11 +316,10 @@
     rows, cols = args[0].shape
     units = units_of(cols)
     count = len(units)
-    width = max(unit[2] for unit in units)
+    slots = diag_slot(units, count - 1) + 1
     big = (8 * rows, cols)
     vmem = pl.BlockSpec(memory_space=pltpu.VMEM)
     hbm = pl.BlockSpec(memory_space=pltpu.HBM)
-    buf = pltpu.VMEM((3, rows, cols), jnp.float32)
     dma = pltpu.SemaphoreType.DMA
     *gathered, factor = pl.pallas_call(
         functools.partial(gather_kernel, total_rows),
@@ -282,15 +328,15 @@
         in_specs=[hbm] * 10,
         out_specs=[vmem] * 4,
         scratch_shapes=[
-            buf, buf, buf,
+            pltpu.VMEM((3, 3, rows, cols), jnp.float32),
             pltpu.VMEM((1, rows), jnp.float32),
             pltpu.VMEM((rows, 128), jnp.float32),
-            pltpu.VMEM((count, 1, width), jnp.float32),
-            pltpu.VMEM((count, 7, 1, width), jnp.float32),
-            dma((count, 3)), dma,
-            dma((count, 7)), dma((count, 7)),
-            dma((count, 2)), dma((count, 2)), dma((count, 2)),
-            dma((3,)), dma((3,)),
+            pltpu.VMEM((3, 1, cols), jnp.float32),
+            pltpu.VMEM((7, 3, 1, cols), jnp.float32),
+            pltpu.VMEM((2, rows // 2, units[0][2]), jnp.float32),
+            dma((4,)), dma, dma, dma((count,)), dma, dma((2,)),
+            dma((count,)), dma((count,)), dma((3,)), dma((3,)),
+            dma((2, slots)), dma((3,)), dma((3,)),
         ],
         compiler_params=pltpu.CompilerParams(
             collective_id=0, has_side_effects=True,

time: 124 us -> 121 us (0.976)
  Pallas kernels: 123 us -> 121 us
    pallas_call x1, Pallas kernels: 114 us -> 112 us  [ringed(): pl.pallas_call(functools.partial(gather_kernel, total_rows), out_shape=[p...]
where the time goes in v1:
time: 121 us
  Pallas kernels  121 us (100%)
    pallas_call x1, Pallas kernels, ringed(): pl.pallas_call(functools.partial(gather_kernel, total_rows), out_shape=[p...  112 us
    pallas_call x1, Pallas kernels, ringed(): pl.pallas_call(write_kernel, out_shape=[ready] * 3 + [line] * 3, in_specs...  9.08 us

profile of v1, /device:TPU:0, one launch (start us, length us, event | category | flops | bytes accessed | tf_op | source)
XLA Modules:
  0.0 121.3 jit_solution(17704563753076029313)
XLA Ops:
  0.6 111.6 %gather.1 = (bf16[4096,1024]{1,0:T(8,128)(2,1)S(1)}, bf16[4096,1024]{1,0:T(8,128)(2,1)S(1)}, bf16[4096,1024]{1,0:T(8,128)(2,1)S(1)}, f32[3,1024]{1,0:T(4,128)S(1)}) custom-call(f32[512,1024]{1,0:T(8,128)} %refs_0_.1, f32[512,1024]{1,0:T(8,128)} %refs_1_.1, f32[512,1024]{1,0:T(8,128)} %refs_2_.1, f32[512,1024]{1,0:T(8,128)} %refs_3_.1, f32[512,1024]{1,0:T(8,128)} %refs_4_.1, ...), custom_call_target="tpu_custom_call" | custom-call | tf_op jit(solution)/shard_map/gather/pallas_call | solution.py:324
  112.2 9.1 %write.1 = (bf16[4096,1024]{1,0:T(8,128)(2,1)}, bf16[4096,1024]{1,0:T(8,128)(2,1)}, bf16[4096,1024]{1,0:T(8,128)(2,1)}, f32[1024]{0:T(1024)}, f32[1024]{0:T(1024)}, /*index=5*/f32[1024]{0:T(1024)}) custom-call(bf16[4096,1024]{1,0:T(8,128)(2,1)S(1)} %get-tuple-element.10.a, bf16[4096,1024]{1,0:T(8,128)(2,1)S(1)} %get-tuple-element.11.b, ...), custom_call_target="tpu_custom_call" | custom-call | tf_op jit(solution)/shard_map/write/pallas_call | solution.py:352

commit v2 on v1

--- a/solution.py
+++ b/solution.py
@@ -12,10 +12,12 @@
 hold_rate = 0.9
 MESH = pl.DeviceIdType.MESH
 UNITS = 8
-PARTS = ((1, 2, 5), (8,), (4, 2, 1, 1))
+PARTS = ((1, 2, 5), (8,), (8,))
+RUNS = (4, 2, 1, 1)
 STEP = 32
-START = 1
+START = 2
 AHEAD = 3
+PIECES = 32
 VMEM_BYTES = 67_043_328
 
 
@@ -61,20 +63,23 @@
     return units
 
 
-def diag_slot(units, u):
-    m = units[u][0]
-    if m < 2:
-        return m
-    return 2 + sum(unit[0] == 2 for unit in units[:u])
+def runs_of(cols):
+    runs = []
+    first = 0
+    for size in RUNS:
+        runs.append((first, size * cols // UNITS))
+        first += size * cols // UNITS
+    return runs
 
 
 def gather_kernel(total_rows, *refs):
     ins, gain_ref = refs[:9], refs[9]
-    outs, factor_ref = refs[10:13], refs[13]
+    outs, factors = refs[10], refs[11:14]
     (
         bufs, gain_line, gain_buf, mine, parts, early,
         load_sem, gain_sem, sum_send, sum_recv, early_send, early_recv,
-        x_recv, y_recv, x_rest, y_rest, diag_recv, chip_recv, send_sem,
+        x_recv, y_recv, x_rest, y_rest, diag_recv, hand_recv, more_recv,
+        chip_recv, send_sem,
     ) = refs[14:]
     w_buf, first_buf, second_buf = (bufs.at[k] for k in range(3))
     rows, cols = bufs.shape[2:]
@@ -93,8 +98,12 @@
         x_near + 1 - 2 * core, y_near + 1 - 2 * core, diag + 1 - 2 * core,
     ]
     units = units_of(cols)
+    runs = runs_of(cols)
     count = len(units)
     early_width = units[0][2]
+    early_rows = half * early_width // cols
+    last_first, last_width = runs[-1]
+    last_rows = rows * last_width // cols
 
     barrier = pltpu.get_barrier_semaphore()
     for peer in peers:
@@ -171,20 +180,29 @@
             ).start()
 
     def block(m, owner, first, tall, c, width):
-        at = pl.ds(pl.multiple_of(owner * rows + first, 16), tall)
-        return outs[m].at[at, pl.ds(c, width)]
-
-    def send(m, ref, recv_sem, peer):
+        at = pl.multiple_of((8 * m + owner) * rows + first, 16)
+        return outs.at[pl.ds(at, tall), pl.ds(c, width)]
+
+    def span(tall):
+        return outs.at[pl.ds(0, tall), :]
+
+    def send(ref, recv_sem, peer):
         pltpu.make_async_remote_copy(
-            src_ref=ref, dst_ref=ref, send_sem=send_sem.at[m], recv_sem=recv_sem,
+            src_ref=ref, dst_ref=ref, send_sem=send_sem, recv_sem=recv_sem,
             device_id={"fsdp": peer}, device_id_type=MESH,
         ).start()
 
     def arrived(ref, recv_sem):
         pltpu.make_async_remote_copy(
-            src_ref=ref, dst_ref=ref, send_sem=send_sem.at[0], recv_sem=recv_sem,
+            src_ref=ref, dst_ref=ref, send_sem=send_sem, recv_sem=recv_sem,
             device_id={"fsdp": partner}, device_id_type=MESH,
         ).wait_recv()
+
+    def left(ref, sem):
+        pltpu.make_async_remote_copy(
+            src_ref=ref, dst_ref=ref, send_sem=sem, recv_sem=chip_recv,
+            device_id={"fsdp": partner}, device_id_type=MESH,
+        ).wait_send()
 
     def early_copy(side, peer):
         return pltpu.make_async_remote_copy(
@@ -196,15 +214,15 @@
 
     def scaled(source, m, owner, lo, hi, c, width):
         scale = jnp.broadcast_to(
-            1.0 / factor_ref[pl.ds(m, 1), pl.ds(c, width)], (16, width)
+            1.0 / factors[m][:, pl.ds(c, width)], (16, width)
         )
 
         def body(i, carry):
             for k in range(STEP // 16):
                 at = pl.multiple_of(i * STEP + k * 16, 16)
                 tile = source[pl.ds(at, 16), pl.ds(c, width)] * scale
-                outs[m][
-                    pl.ds(pl.multiple_of(owner * rows + at, 16), 16),
+                outs[
+                    pl.ds(pl.multiple_of((8 * m + owner) * rows + at, 16), 16),
                     pl.ds(c, width),
                 ] = tile.astype(jnp.bfloat16)
             return carry
@@ -218,20 +236,33 @@
         total = mine[m, :, at]
         for slot in range(7):
             total = total + parts[slot, m, :, at]
-        factor_ref[pl.ds(m, 1), at] = total / total_rows
+        factors[m][:, at] = total / total_rows
         for h in (1, 0):
             scaled(w_buf.at[m], m, me, h * half, (h + 1) * half, c, width)
             if u == 0 and h == 0:
                 continue
             ref = block(m, me, h * half, half, c, width)
-            send(m, ref, x_recv.at[u] if h == 0 else x_rest.at[m], x_near)
-            send(m, ref, y_recv.at[u] if h == 1 else y_rest.at[m], y_near)
-        send(m, block(m, me, 0, rows, c, width), chip_recv.at[m], partner)
+            near, rest = (x_near, y_near) if h == 0 else (y_near, x_near)
+            recv, rest_recv = (x_recv, y_rest) if h == 0 else (y_recv, x_rest)
+            send(ref, rest_recv, rest)
+            if m < 2:
+                send(ref, recv.at[0], near)
+            else:
+                for r, (first, wide) in enumerate(runs):
+                    send(
+                        block(m, me, h * half, half, first, wide),
+                        recv.at[1 + r], near,
+                    )
+        send(block(m, me, 0, rows, c, width), chip_recv, partner)
 
     def take_early():
         for side, owner in enumerate((x_near, y_near)):
             arrived(early.at[side], early_recv.at[side])
             scaled(early.at[side], 0, owner, 0, half, 0, early_width)
+
+    def pass_on(ref, slot, h, near):
+        send(ref, diag_recv.at[h, slot], near)
+        send(ref, chip_recv, partner)
 
     sums(0)
     pl.semaphore_wait(barrier, 7)
@@ -240,91 +271,123 @@
     send_sums(1)
     early_copy(0, x_near).start()
     early_copy(1, y_near).start()
-    for u in range(2, count + 2):
-        if u < count:
-            sums(u)
-            send_sums(u)
-        finish(u - 2)
-        if u == 3:
-            take_early()
-
-    for u, (m, c, width) in enumerate(units):
-        ref = block(m, x_near, 0, half, c, width)
-        if u > 0:
-            arrived(ref, x_recv.at[u])
-        send(m, ref, diag_recv.at[0, diag_slot(units, u)], y_near)
-        send(m, ref, chip_recv.at[m], partner)
-        ref = block(m, y_near, half, half, c, width)
-        arrived(ref, y_recv.at[u])
-        send(m, ref, diag_recv.at[1, diag_slot(units, u)], x_near)
-        send(m, ref, chip_recv.at[m], partner)
-        if c + width == cols:
-            ref = block(m, x_near, half, half, 0, cols)
-            arrived(ref, x_rest.at[m])
-            send(m, ref, chip_recv.at[m], partner)
-            skip = early_width if m == 0 else 0
-            arrived(
-                block(m, y_near, 0, half, skip, cols - skip), y_rest.at[m]
-            )
-            ref = block(m, y_near, 0, half, 0, cols)
-            send(m, ref, chip_recv.at[m], partner)
-    for u, (m, c, width) in enumerate(units):
-        if m < 2:
-            if c + width < cols:
-                continue
-            c, width = 0, cols
+    sums(2)
+    send_sums(2)
+    finish(0)
+    finish(1)
+    take_early()
+    for u in range(3, count):
+        sums(u)
+        send_sums(u)
+        finish(u - 1)
+    finish(count - 1)
+
+    arrived(span(2 * half - early_rows), x_recv.at[0])
+    arrived(span(2 * half), y_recv.at[0])
+    for m in range(2):
+        pass_on(block(m, x_near, 0, half, 0, cols), 0, 0, y_near)
+        pass_on(block(m, y_near, half, half, 0, cols), 0, 1, x_near)
+    for r, (c, width) in enumerate(runs[:-1]):
+        ref = block(2, x_near, 0, half, c, width)
+        arrived(ref, x_recv.at[1 + r])
+        pass_on(ref, 1 + r, 0, y_near)
+        ref = block(2, y_near, half, half, c, width)
+        arrived(ref, y_recv.at[1 + r])
+        pass_on(ref, 1 + r, 1, x_near)
+
+    slot = len(runs)
+    x_last = block(2, x_near, 0, half, last_first, last_width)
+    y_last = block(2, y_near, half, half, last_first, last_width)
+    arrived(x_last, x_recv.at[slot])
+    arrived(y_last, y_recv.at[slot])
+
+    @pl.when(core == 0)
+    def _():
+        send(x_last, hand_recv.at[0], partner)
+        send(y_last, hand_recv.at[1], partner)
+
+    @pl.when(core == 1)
+    def _():
+        pass_on(x_last, slot, 0, y_near)
+        pass_on(y_last, slot, 1, x_near)
+        ref = block(2, x_near - 1, 0, half, last_first, last_width)
+        arrived(ref, hand_recv.at[0])
+        send(ref, more_recv.at[0], y_near)
+        ref = block(2, y_near - 1, half, half, last_first, last_width)
+        arrived(ref, hand_recv.at[1])
+        send(ref, more_recv.at[1], x_near)
+
+    arrived(span(3 * half), x_rest)
+    arrived(span(3 * half - early_rows), y_rest)
+    for m in range(3):
+        send(block(m, x_near, half, half, 0, cols), chip_recv, partner)
+        send(block(m, y_near, 0, half, 0, cols), chip_recv, partner)
+
+    for h in range(2):
+        arrived(span(2 * half), diag_recv.at[h, 0])
+        for m in range(2):
+            send(block(m, diag, h * half, half, 0, cols), chip_recv, partner)
+    for r, (c, width) in enumerate(runs[:-1]):
         for h in range(2):
-            ref = block(m, diag, h * half, half, c, width)
-            arrived(ref, diag_recv.at[h, diag_slot(units, u)])
-            send(m, ref, chip_recv.at[m], partner)
-
-    for m in range(3):
-        taken = outs[m].at[pl.ds(0, 4 * rows), :]
-        early_rows = rows * early_width // cols if m == 0 else 0
-        sent = outs[m].at[pl.ds(0, 7 * rows - early_rows), :]
-        arrived(taken, chip_recv.at[m])
-        pltpu.make_async_remote_copy(
-            src_ref=sent, dst_ref=sent, send_sem=send_sem.at[m],
-            recv_sem=chip_recv.at[m], device_id={"fsdp": partner},
-            device_id_type=MESH,
-        ).wait_send()
-    for ref, sem in ((parts, sum_send), (early, early_send)):
-        pltpu.make_async_remote_copy(
-            src_ref=ref, dst_ref=ref, send_sem=sem, recv_sem=sum_recv.at[0],
-            device_id={"fsdp": partner}, device_id_type=MESH,
-        ).wait_send()
-
-
-def write_kernel(a, b, c, factor, out_a, out_b, out_c, fa, fb, fc, sem):
-    copies = []
-    for k, (src, dst) in enumerate(((a, out_a), (b, out_b), (c, out_c))):
-        rows = src.shape[0] // 4
-        for p in range(4):
-            at = pl.ds(p * rows, rows)
-            copies.append(
-                pltpu.make_async_copy(src.at[at, :], dst.at[at, :], sem.at[k, p])
-            )
-    for copy in copies:
-        copy.start()
-    for m, out in enumerate((fa, fb, fc)):
-        out[...] = factor[m, :]
-    for copy in copies:
-        copy.wait()
+            ref = block(2, diag, h * half, half, c, width)
+            arrived(ref, diag_recv.at[h, 1 + r])
+            send(ref, chip_recv, partner)
+
+    @pl.when(core == 0)
+    def _():
+        arrived(span(12 * rows + last_rows), chip_recv)
+        left(span(21 * rows - 2 * early_rows - 2 * last_rows), send_sem)
+
+    @pl.when(core == 1)
+    def _():
+        for owner, recv in ((diag, diag_recv.at[:, slot]), (diag - 1, more_recv)):
+            for h in range(2):
+                ref = block(2, owner, h * half, half, last_first, last_width)
+                arrived(ref, recv.at[h])
+                send(ref, chip_recv, partner)
+        arrived(span(12 * rows - 2 * last_rows), chip_recv)
+        left(span(21 * rows - 2 * early_rows + 2 * last_rows), send_sem)
+
+    left(parts, sum_send)
+    left(early, early_send)
+
+
+def write_kernel(*refs):
+    src, outs, sem = refs[0], refs[4:7], refs[10]
+    lines = [
+        pltpu.make_async_copy(refs[1 + k], refs[7 + k], sem.at[3 + k])
+        for k in range(3)
+    ]
+    for line in lines:
+        line.start()
+    tall = outs[0].shape[0]
+    step = tall // PIECES
+    for k in range(3):
+        for p in range(PIECES):
+            pltpu.make_async_copy(
+                src.at[pl.ds(k * tall + p * step, step), :],
+                outs[k].at[pl.ds(p * step, step), :], sem.at[k],
+            ).start()
+    for k in range(3):
+        whole = src.at[pl.ds(k * tall, tall), :]
+        pltpu.make_async_copy(whole, outs[k], sem.at[k]).wait()
+    for line in lines:
+        line.wait()
 
 
 def ringed(*args, total_rows):
     rows, cols = args[0].shape
     units = units_of(cols)
     count = len(units)
-    slots = diag_slot(units, count - 1) + 1
+    slots = len(RUNS) + 1
     big = (8 * rows, cols)
     vmem = pl.BlockSpec(memory_space=pltpu.VMEM)
     hbm = pl.BlockSpec(memory_space=pltpu.HBM)
     dma = pltpu.SemaphoreType.DMA
-    *gathered, factor = pl.pallas_call(
+    gathered = pl.pallas_call(
         functools.partial(gather_kernel, total_rows),
-        out_shape=[pltpu.VMEM(big, jnp.bfloat16)] * 3
-        + [pltpu.VMEM((3, cols), jnp.float32)],
+        out_shape=[pltpu.VMEM((24 * rows, cols), jnp.bfloat16)]
+        + [pltpu.VMEM((1, cols), jnp.float32)] * 3,
         in_specs=[hbm] * 10,
         out_specs=[vmem] * 4,
         scratch_shapes=[
@@ -335,8 +398,8 @@
             pltpu.VMEM((7, 3, 1, cols), jnp.float32),
             pltpu.VMEM((2, rows // 2, units[0][2]), jnp.float32),
             dma((4,)), dma, dma, dma((count,)), dma, dma((2,)),
-            dma((count,)), dma((count,)), dma((3,)), dma((3,)),
-            dma((2, slots)), dma((3,)), dma((3,)),
+            dma((slots,)), dma((slots,)), dma, dma,
+            dma((2, slots)), dma((2,)), dma((2,)), dma, dma,
         ],
         compiler_params=pltpu.CompilerParams(
             collective_id=0, has_side_effects=True,
@@ -348,16 +411,17 @@
         for a in (*args[:9], args[9].reshape(1, rows))
     ))
     ready = jax.ShapeDtypeStruct(big, jnp.bfloat16)
-    line = jax.ShapeDtypeStruct((cols,), jnp.float32)
-    return pl.pallas_call(
+    line = jax.ShapeDtypeStruct((1, cols), jnp.float32)
+    *ready, a, b, c = pl.pallas_call(
         write_kernel,
         out_shape=[ready] * 3 + [line] * 3,
         in_specs=[vmem] * 4,
-        out_specs=[hbm] * 3 + [vmem] * 3,
-        scratch_shapes=[dma((3, 4))],
+        out_specs=[hbm] * 6,
+        scratch_shapes=[dma((6,))],
         compiler_params=pltpu.CompilerParams(vmem_limit_bytes=2**20),
         name="write",
-    )(*gathered, factor)
+    )(*gathered)
+    return ready + [f.reshape(cols) for f in (a, b, c)]
 
 
 def on_device(*args, devices):

time: 121 us -> 120 us (level)
  Pallas kernels: 121 us -> 119 us
where the time goes in v2:
time: 120 us; the launch traced here: 119 us
  Pallas kernels  119 us (99%)
    pallas_call x1, Pallas kernels, ringed(): pl.pallas_call(functools.partial(gather_kernel, total_rows), out_shape=[p...  110 us
    pallas_call x1, Pallas kernels, ringed(): pl.pallas_call(write_kernel, out_shape=[ready] * 3 + [line] * 3, in_specs...  8.34 us

profile of v2, /device:TPU:0, one launch (start us, length us, event | category | flops | bytes accessed | tf_op | source)
XLA Modules:
  0.0 119.4 jit_solution(237031356544438826)
XLA Ops:
  0.6 110.4 %gather.1 = (bf16[12288,1024]{1,0:T(8,128)(2,1)S(1)}, f32[1,1024]{1,0:T(1,128)S(1)}, f32[1,1024]{1,0:T(1,128)S(1)}, f32[1,1024]{1,0:T(1,128)S(1)}) custom-call(f32[512,1024]{1,0:T(8,128)} %refs_0_.1, f32[512,1024]{1,0:T(8,128)} %refs_1_.1, f32[512,1024]{1,0:T(8,128)} %refs_2_.1, f32[512,1024]{1,0:T(8,128)} %refs_3_.1, f32[512,1024]{1,0:T(8,128)} %refs_4_.1, ...), custom_call_target="tpu_custom_call" | custom-call | tf_op jit(solution)/shard_map/gather/pallas_call | solution.py:387
  111.1 8.3 %write.1 = (bf16[4096,1024]{1,0:T(8,128)(2,1)}, bf16[4096,1024]{1,0:T(8,128)(2,1)}, bf16[4096,1024]{1,0:T(8,128)(2,1)}, f32[1,1024]{1,0:T(1,128)}, f32[1,1024]{1,0:T(1,128)}, /*index=5*/f32[1,1024]{1,0:T(1,128)}) custom-call(bf16[12288,1024]{1,0:T(8,128)(2,1)S(1)} %get-tuple-element.16.refs_0_, f32[1,1024]{1,0:T(1,128)S(1)} %get-tuple-element.17.refs_1_, ...), custom_call_target="tpu_custom_call" | custom-call | tf_op jit(solution)/shard_map/write/pallas_call | solution.py:415

commit v3 on v2

--- a/solution.py
+++ b/solution.py
@@ -13,7 +13,8 @@
 MESH = pl.DeviceIdType.MESH
 UNITS = 8
 PARTS = ((1, 2, 5), (8,), (8,))
-RUNS = (4, 2, 1, 1)
+KEY_RUNS = (4, 2, 2)
+VALUE_RUNS = (2, 2, 2, 1, 1)
 STEP = 32
 START = 2
 AHEAD = 3
@@ -63,28 +64,16 @@
     return units
 
 
-def runs_of(cols):
+def runs_of(sizes, cols):
     runs = []
     first = 0
-    for size in RUNS:
+    for size in sizes:
         runs.append((first, size * cols // UNITS))
         first += size * cols // UNITS
     return runs
 
 
-def gather_kernel(total_rows, *refs):
-    ins, gain_ref = refs[:9], refs[9]
-    outs, factors = refs[10], refs[11:14]
-    (
-        bufs, gain_line, gain_buf, mine, parts, early,
-        load_sem, gain_sem, sum_send, sum_recv, early_send, early_recv,
-        x_recv, y_recv, x_rest, y_rest, diag_recv, hand_recv, more_recv,
-        chip_recv, send_sem,
-    ) = refs[14:]
-    w_buf, first_buf, second_buf = (bufs.at[k] for k in range(3))
-    rows, cols = bufs.shape[2:]
-    half = rows // 2
-
+def places():
     me = lax.axis_index("fsdp")
     core = me % 2
     x = (me // 2) % 2
@@ -93,17 +82,32 @@
     x_near = me + 2 - 4 * x
     y_near = me + 4 - 8 * y
     diag = x_near + 4 - 8 * y
+    return me, core, partner, x_near, y_near, diag
+
+
+def gather_kernel(total_rows, *refs):
+    ins, gain_ref = refs[:9], refs[9]
+    outs, value, factors = refs[10], refs[11], refs[12:15]
+    (
+        bufs, gain_line, gain_buf, mine, parts, early,
+        load_sem, gain_sem, sum_send, sum_recv, early_send, early_recv,
+        x_recv, y_recv, x_rest, y_rest, diag_recv, x_value, y_value,
+        chip_recv, chip_value, send_sem,
+    ) = refs[15:]
+    w_buf, first_buf, second_buf = (bufs.at[k] for k in range(3))
+    rows, cols = bufs.shape[2:]
+    half = rows // 2
+
+    me, core, partner, x_near, y_near, diag = places()
     peers = [
-        partner, x_near, y_near, diag,
-        x_near + 1 - 2 * core, y_near + 1 - 2 * core, diag + 1 - 2 * core,
+        diag + 1 - 2 * core, diag, x_near + 1 - 2 * core, y_near + 1 - 2 * core,
+        x_near, y_near, partner,
     ]
     units = units_of(cols)
-    runs = runs_of(cols)
+    runs = runs_of(KEY_RUNS, cols)
     count = len(units)
     early_width = units[0][2]
     early_rows = half * early_width // cols
-    last_first, last_width = runs[-1]
-    last_rows = rows * last_width // cols
 
     barrier = pltpu.get_barrier_semaphore()
     for peer in peers:
@@ -180,8 +184,12 @@
             ).start()
 
     def block(m, owner, first, tall, c, width):
-        at = pl.multiple_of((8 * m + owner) * rows + first, 16)
-        return outs.at[pl.ds(at, tall), pl.ds(c, width)]
+        ref = value if m == 2 else outs
+        at = owner * rows + first
+        if m == 1:
+            at = at + 8 * rows
+        at = pl.multiple_of(at, 16)
+        return ref.at[pl.ds(at, tall), pl.ds(c, width)]
 
     def span(tall):
         return outs.at[pl.ds(0, tall), :]
@@ -221,10 +229,7 @@
             for k in range(STEP // 16):
                 at = pl.multiple_of(i * STEP + k * 16, 16)
                 tile = source[pl.ds(at, 16), pl.ds(c, width)] * scale
-                outs[
-                    pl.ds(pl.multiple_of((8 * m + owner) * rows + at, 16), 16),
-                    pl.ds(c, width),
-                ] = tile.astype(jnp.bfloat16)
+                block(m, owner, at, 16, c, width)[...] = tile.astype(jnp.bfloat16)
             return carry
 
         lax.fori_loop(lo // STEP, hi // STEP, body, 0)
@@ -239,30 +244,20 @@
         factors[m][:, at] = total / total_rows
         for h in (1, 0):
             scaled(w_buf.at[m], m, me, h * half, (h + 1) * half, c, width)
-            if u == 0 and h == 0:
+            if m == 2 or u == 0 and h == 0:
                 continue
             ref = block(m, me, h * half, half, c, width)
-            near, rest = (x_near, y_near) if h == 0 else (y_near, x_near)
-            recv, rest_recv = (x_recv, y_rest) if h == 0 else (y_recv, x_rest)
-            send(ref, rest_recv, rest)
-            if m < 2:
-                send(ref, recv.at[0], near)
-            else:
-                for r, (first, wide) in enumerate(runs):
-                    send(
-                        block(m, me, h * half, half, first, wide),
-                        recv.at[1 + r], near,
-                    )
-        send(block(m, me, 0, rows, c, width), chip_recv, partner)
+            send(ref, x_recv.at[m] if h == 0 else x_rest, x_near)
+            send(ref, y_recv.at[m] if h == 1 else y_rest, y_near)
+        send(
+            block(m, me, 0, rows, c, width),
+            chip_value if m == 2 else chip_recv, partner,
+        )
 
     def take_early():
         for side, owner in enumerate((x_near, y_near)):
             arrived(early.at[side], early_recv.at[side])
             scaled(early.at[side], 0, owner, 0, half, 0, early_width)
-
-    def pass_on(ref, slot, h, near):
-        send(ref, diag_recv.at[h, slot], near)
-        send(ref, chip_recv, partner)
 
     sums(0)
     pl.semaphore_wait(barrier, 7)
@@ -282,114 +277,218 @@
         finish(u - 1)
     finish(count - 1)
 
-    arrived(span(2 * half - early_rows), x_recv.at[0])
-    arrived(span(2 * half), y_recv.at[0])
     for m in range(2):
-        pass_on(block(m, x_near, 0, half, 0, cols), 0, 0, y_near)
-        pass_on(block(m, y_near, half, half, 0, cols), 0, 1, x_near)
-    for r, (c, width) in enumerate(runs[:-1]):
-        ref = block(2, x_near, 0, half, c, width)
-        arrived(ref, x_recv.at[1 + r])
-        pass_on(ref, 1 + r, 0, y_near)
-        ref = block(2, y_near, half, half, c, width)
-        arrived(ref, y_recv.at[1 + r])
-        pass_on(ref, 1 + r, 1, x_near)
-
-    slot = len(runs)
-    x_last = block(2, x_near, 0, half, last_first, last_width)
-    y_last = block(2, y_near, half, half, last_first, last_width)
-    arrived(x_last, x_recv.at[slot])
-    arrived(y_last, y_recv.at[slot])
+        arrived(span(half - early_rows * (m == 0)), x_recv.at[m])
+        arrived(span(half), y_recv.at[m])
+        pieces = enumerate(runs) if m == 1 else [(-1, (0, cols))]
+        for r, (c, width) in pieces:
+            send(
+                block(m, x_near, 0, half, c, width), diag_recv.at[0, 1 + r], y_near
+            )
+            send(
+                block(m, y_near, half, half, c, width), diag_recv.at[1, 1 + r],
+                x_near,
+            )
+
+    mine_value = block(2, me, 0, rows, 0, cols)
 
     @pl.when(core == 0)
     def _():
-        send(x_last, hand_recv.at[0], partner)
-        send(y_last, hand_recv.at[1], partner)
+        send(mine_value, x_value, x_near)
+        send(mine_value, y_value, y_near)
+
+    arrived(span(2 * half), x_rest)
+    arrived(span(2 * half - early_rows), y_rest)
+    for m in range(2):
+        send(block(m, x_near, 0, rows, 0, cols), chip_recv, partner)
+        send(block(m, y_near, 0, rows, 0, cols), chip_recv, partner)
+    for m in range(2):
+        pieces = enumerate(runs) if m == 1 else [(-1, (0, cols))]
+        for r, (c, width) in pieces:
+            for h in range(2):
+                ref = block(m, diag, h * half, half, c, width)
+                arrived(ref, diag_recv.at[h, 1 + r])
+                send(ref, chip_recv, partner)
+    arrived(span(8 * rows), chip_recv)
+    arrived(span(rows), chip_value)
+
+    @pl.when(core == 0)
+    def _():
+        arrived(span(rows), x_value)
+        arrived(span(rows), y_value)
+        left(span(15 * rows - 2 * early_rows), send_sem)
+        left(span(2 * rows), send_sem)
 
     @pl.when(core == 1)
     def _():
-        pass_on(x_last, slot, 0, y_near)
-        pass_on(y_last, slot, 1, x_near)
-        ref = block(2, x_near - 1, 0, half, last_first, last_width)
-        arrived(ref, hand_recv.at[0])
-        send(ref, more_recv.at[0], y_near)
-        ref = block(2, y_near - 1, half, half, last_first, last_width)
-        arrived(ref, hand_recv.at[1])
-        send(ref, more_recv.at[1], x_near)
-
-    arrived(span(3 * half), x_rest)
-    arrived(span(3 * half - early_rows), y_rest)
-    for m in range(3):
-        send(block(m, x_near, half, half, 0, cols), chip_recv, partner)
-        send(block(m, y_near, 0, half, 0, cols), chip_recv, partner)
-
-    for h in range(2):
-        arrived(span(2 * half), diag_recv.at[h, 0])
-        for m in range(2):
-            send(block(m, diag, h * half, half, 0, cols), chip_recv, partner)
-    for r, (c, width) in enumerate(runs[:-1]):
-        for h in range(2):
-            ref = block(2, diag, h * half, half, c, width)
-            arrived(ref, diag_recv.at[h, 1 + r])
-            send(ref, chip_recv, partner)
-
-    @pl.when(core == 0)
-    def _():
-        arrived(span(12 * rows + last_rows), chip_recv)
-        left(span(21 * rows - 2 * early_rows - 2 * last_rows), send_sem)
-
-    @pl.when(core == 1)
-    def _():
-        for owner, recv in ((diag, diag_recv.at[:, slot]), (diag - 1, more_recv)):
-            for h in range(2):
-                ref = block(2, owner, h * half, half, last_first, last_width)
-                arrived(ref, recv.at[h])
-                send(ref, chip_recv, partner)
-        arrived(span(12 * rows - 2 * last_rows), chip_recv)
-        left(span(21 * rows - 2 * early_rows + 2 * last_rows), send_sem)
+        left(span(15 * rows - 2 * early_rows), send_sem)
 
     left(parts, sum_send)
     left(early, early_send)
 
 
-def write_kernel(*refs):
-    src, outs, sem = refs[0], refs[4:7], refs[10]
-    lines = [
-        pltpu.make_async_copy(refs[1 + k], refs[7 + k], sem.at[3 + k])
+def value_kernel(held, token, value, *sems):
+    (
+        x_recv, y_recv, x_rest, y_rest, diag_recv, chip_recv, send_sem, ready,
+    ) = sems
+    cols = held.shape[1]
+    rows = held.shape[0] // 8
+    half = rows // 2
+    me, core, partner, x_near, y_near, diag = places()
+    runs = runs_of(VALUE_RUNS, cols)
+
+    barrier = pltpu.get_barrier_semaphore()
+    for peer in (x_near, y_near):
+        pl.semaphore_signal(
+            barrier, inc=1, device_id={"fsdp": peer}, device_id_type=MESH
+        )
+
+    @pl.when(core == 1)
+    def _():
+        pl.semaphore_signal(
+            barrier, inc=1, device_id={"fsdp": partner}, device_id_type=MESH
+        )
+
+    pl.semaphore_wait(barrier, 3 - core)
+
+    def block(ref, owner, first, tall, c, width):
+        at = pl.multiple_of(owner * rows + first, 16)
+        return ref.at[pl.ds(at, tall), pl.ds(c, width)]
+
+    def send(source, owner, first, tall, c, width, recv_sem, peer):
+        pltpu.make_async_remote_copy(
+            src_ref=block(source, owner, first, tall, c, width),
+            dst_ref=block(value, owner, first, tall, c, width),
+            send_sem=send_sem, recv_sem=recv_sem,
+            device_id={"fsdp": peer}, device_id_type=MESH,
+        ).start()
+
+    def copy_of(ref, recv_sem):
+        return pltpu.make_async_remote_copy(
+            src_ref=ref, dst_ref=ref, send_sem=send_sem, recv_sem=recv_sem,
+            device_id={"fsdp": partner}, device_id_type=MESH,
+        )
+
+    def forward(source, r, c, width):
+        send(source, x_near, 0, half, c, width, diag_recv.at[0, r], y_near)
+        send(source, y_near, half, half, c, width, diag_recv.at[1, r], x_near)
+
+    def cross(source):
+        for owner in (x_near, y_near):
+            send(source, owner, 0, rows, 0, cols, chip_recv, partner)
+
+    @pl.when(core == 0)
+    def _():
+        pl.semaphore_signal(
+            ready, inc=1, device_id={"fsdp": partner}, device_id_type=MESH
+        )
+        for r, (c, width) in enumerate(runs):
+            forward(held, r, c, width)
+        cross(held)
+
+    @pl.when(core == 1)
+    def _():
+        for r, (c, width) in enumerate(runs):
+            send(held, me, 0, half, c, width, x_recv.at[r], x_near)
+            send(held, me, half, half, c, width, y_recv.at[r], y_near)
+        send(held, me, half, half, 0, cols, x_rest, x_near)
+        send(held, me, 0, half, 0, cols, y_rest, y_near)
+        for r, (c, width) in enumerate(runs):
+            copy_of(block(value, x_near, 0, half, c, width), x_recv.at[r]).wait_recv()
+            copy_of(
+                block(value, y_near, half, half, c, width), y_recv.at[r]
+            ).wait_recv()
+            forward(value, r, c, width)
+        copy_of(block(value, x_near, half, half, 0, cols), x_rest).wait_recv()
+        copy_of(block(value, y_near, 0, half, 0, cols), y_rest).wait_recv()
+        pl.semaphore_wait(ready, 1)
+        cross(value)
+
+    for r, (c, width) in enumerate(runs):
+        for h in range(2):
+            copy_of(
+                block(value, diag, h * half, half, c, width), diag_recv.at[h, r]
+            ).wait_recv()
+            send(value, diag, h * half, half, c, width, chip_recv, partner)
+    copy_of(value.at[pl.ds(0, 3 * rows), :], chip_recv).wait_recv()
+
+    @pl.when(core == 0)
+    def _():
+        copy_of(value.at[pl.ds(0, 4 * rows), :], chip_recv).wait_send()
+
+    @pl.when(core == 1)
+    def _():
+        copy_of(value.at[pl.ds(0, 6 * rows), :], chip_recv).wait_send()
+
+
+def write_pair(src, *refs):
+    lines, outs, line_outs, sem = refs[:3], refs[3:5], refs[5:8], refs[8]
+    copies = [
+        pltpu.make_async_copy(lines[k], line_outs[k], sem.at[2 + k])
         for k in range(3)
     ]
-    for line in lines:
-        line.start()
+    for copy in copies:
+        copy.start()
     tall = outs[0].shape[0]
     step = tall // PIECES
-    for k in range(3):
+    for k in range(2):
         for p in range(PIECES):
             pltpu.make_async_copy(
                 src.at[pl.ds(k * tall + p * step, step), :],
                 outs[k].at[pl.ds(p * step, step), :], sem.at[k],
             ).start()
-    for k in range(3):
+    for k in range(2):
         whole = src.at[pl.ds(k * tall, tall), :]
         pltpu.make_async_copy(whole, outs[k], sem.at[k]).wait()
-    for line in lines:
-        line.wait()
+    for copy in copies:
+        copy.wait()
+
+
+def write_value(held, value, out, sem):
+    rows = out.shape[0] // 8
+    me, core, _, x_near, y_near, diag = places()
+    step = 8 * rows // PIECES
+
+    def put(src, first):
+        for p in range(rows // step):
+            at = pl.ds(pl.multiple_of(first * rows + p * step, 16), step)
+            pltpu.make_async_copy(src.at[at, :], out.at[at, :], sem).start()
+
+    for k in range(2):
+        put(held, me - core + k)
+        put(value, diag - core + k)
+    for near in (x_near, y_near):
+        put(value, near + 1 - 2 * core)
+
+    @pl.when(core == 0)
+    def _():
+        put(held, x_near)
+        put(held, y_near)
+
+    @pl.when(core == 1)
+    def _():
+        put(value, x_near)
+        put(value, y_near)
+
+    pltpu.make_async_copy(value, out, sem).wait()
 
 
 def ringed(*args, total_rows):
     rows, cols = args[0].shape
     units = units_of(cols)
     count = len(units)
-    slots = len(RUNS) + 1
-    big = (8 * rows, cols)
     vmem = pl.BlockSpec(memory_space=pltpu.VMEM)
     hbm = pl.BlockSpec(memory_space=pltpu.HBM)
     dma = pltpu.SemaphoreType.DMA
-    gathered = pl.pallas_call(
+    held = pltpu.VMEM((8 * rows, cols), jnp.bfloat16)
+    runs = len(VALUE_RUNS)
+    slots = len(KEY_RUNS) + 1
+    pair, held_value, *factors = pl.pallas_call(
         functools.partial(gather_kernel, total_rows),
-        out_shape=[pltpu.VMEM((24 * rows, cols), jnp.bfloat16)]
+        out_shape=[pltpu.VMEM((16 * rows, cols), jnp.bfloat16), held]
         + [pltpu.VMEM((1, cols), jnp.float32)] * 3,
         in_specs=[hbm] * 10,
-        out_specs=[vmem] * 4,
+        out_specs=[vmem] * 5,
         scratch_shapes=[
             pltpu.VMEM((3, 3, rows, cols), jnp.float32),
             pltpu.VMEM((1, rows), jnp.float32),
@@ -398,8 +497,8 @@
             pltpu.VMEM((7, 3, 1, cols), jnp.float32),
             pltpu.VMEM((2, rows // 2, units[0][2]), jnp.float32),
             dma((4,)), dma, dma, dma((count,)), dma, dma((2,)),
-            dma((slots,)), dma((slots,)), dma, dma,
-            dma((2, slots)), dma((2,)), dma((2,)), dma, dma,
+            dma((2,)), dma((2,)), dma, dma, dma((2, slots)), dma, dma,
+            dma, dma, dma,
         ],
         compiler_params=pltpu.CompilerParams(
             collective_id=0, has_side_effects=True,
@@ -410,18 +509,43 @@
         pltpu.with_memory_space_constraint(a, pltpu.HBM)
         for a in (*args[:9], args[9].reshape(1, rows))
     ))
-    ready = jax.ShapeDtypeStruct(big, jnp.bfloat16)
+    ready = jax.ShapeDtypeStruct((8 * rows, cols), jnp.bfloat16)
     line = jax.ShapeDtypeStruct((1, cols), jnp.float32)
-    *ready, a, b, c = pl.pallas_call(
-        write_kernel,
-        out_shape=[ready] * 3 + [line] * 3,
+    query, key, *lines = pl.pallas_call(
+        write_pair,
+        out_shape=[ready] * 2 + [line] * 3,
         in_specs=[vmem] * 4,
-        out_specs=[hbm] * 6,
-        scratch_shapes=[dma((6,))],
+        out_specs=[hbm] * 5,
+        scratch_shapes=[dma((5,))],
+        compiler_params=pltpu.CompilerParams(
+            has_side_effects=True, vmem_limit_bytes=2**20
+        ),
+        name="write_pair",
+    )(pair, *factors)
+    value = pl.pallas_call(
+        value_kernel,
+        out_shape=held,
+        in_specs=[vmem, hbm],
+        out_specs=vmem,
+        scratch_shapes=[
+            dma((runs,)), dma((runs,)), dma, dma, dma((2, runs)), dma, dma,
+            pltpu.SemaphoreType.REGULAR,
+        ],
+        compiler_params=pltpu.CompilerParams(
+            collective_id=1, has_side_effects=True, vmem_limit_bytes=2**20
+        ),
+        name="value",
+    )(held_value, pltpu.with_memory_space_constraint(lines[0], pltpu.HBM))
+    value = pl.pallas_call(
+        write_value,
+        out_shape=ready,
+        in_specs=[vmem] * 2,
+        out_specs=hbm,
+        scratch_shapes=[dma],
         compiler_params=pltpu.CompilerParams(vmem_limit_bytes=2**20),
-        name="write",
-    )(*gathered)
-    return ready + [f.reshape(cols) for f in (a, b, c)]
+        name="write_value",
+    )(held_value, value)
+    return [query, key, value] + [f.reshape(cols) for f in lines]
 
 
 def on_device(*args, devices):

time: 120 us -> 114 us (0.950)
  Pallas kernels: 119 us -> 114 us
    pallas_call x1, Pallas kernels: 110 us -> 88.1 us  [ringed(): pl.pallas_call(functools.partial(gather_kernel, total_rows), out_shape=[p...]
    pallas_call x1 -> x3, Pallas kernels: 8.34 us -> 25.4 us  [the longest x1 16.3 us: ringed(): pl.pallas_call(value_kernel, out_shape=held, in_specs=[vmem, hbm], out_sp...]
where the time goes in v3:
time: 114 us
  Pallas kernels  114 us (100%)
    pallas_call x1, Pallas kernels, ringed(): pl.pallas_call(functools.partial(gather_kernel, total_rows), out_shape=[p...  88.1 us
    pallas_call x1, Pallas kernels, ringed(): pl.pallas_call(value_kernel, out_shape=held, in_specs=[vmem, hbm], out_sp...  16.3 us
    pallas_call x1, Pallas kernels, ringed(): pl.pallas_call(write_pair, out_shape=[ready] * 2 + [line] * 3, in_specs=[...  5.82 us
    pallas_call x1, Pallas kernels, ringed(): pl.pallas_call(write_value, out_shape=ready, in_specs=[vmem] * 2, out_spe...  3.28 us

profile of v3, /device:TPU:0, one launch (start us, length us, event | category | flops | bytes accessed | tf_op | source)
XLA Modules:
  0.0 114.2 jit_solution(9328555664802692182)
XLA Ops:
  0.6 88.1 %gather.1 = (bf16[8192,1024]{1,0:T(8,128)(2,1)S(1)}, bf16[4096,1024]{1,0:T(8,128)(2,1)S(1)}, f32[1,1024]{1,0:T(1,128)S(1)}, f32[1,1024]{1,0:T(1,128)S(1)}, f32[1,1024]{1,0:T(1,128)S(1)}) custom-call(f32[512,1024]{1,0:T(8,128)} %refs_0_.1, f32[512,1024]{1,0:T(8,128)} %refs_1_.1, f32[512,1024]{1,0:T(8,128)} %refs_2_.1, f32[512,1024]{1,0:T(8,128)} %refs_3_.1, ...), custom_call_target="tpu_custom_call" | custom-call | tf_op jit(solution)/shard_map/gather/pallas_call | solution.py:486
  88.8 5.8 %write_pair.1 = (bf16[4096,1024]{1,0:T(8,128)(2,1)}, bf16[4096,1024]{1,0:T(8,128)(2,1)}, f32[1,1024]{1,0:T(1,128)}, f32[1,1024]{1,0:T(1,128)}, f32[1,1024]{1,0:T(1,128)}) custom-call(bf16[8192,1024]{1,0:T(8,128)(2,1)S(1)} %get-tuple-element.16.src, f32[1,1024]{1,0:T(1,128)S(1)} %get-tuple-element.17.refs_0_, f32[1,1024]{1,0:T(1,128)S(1)} %get-tuple-element.18.refs_1_, ...), custom_call_target="tpu_custom_call" | custom-call | tf_op jit(solution)/shard_map/write_pair/pallas_call | solution.py:514
  94.6 16.3 %value.1 = bf16[4096,1024]{1,0:T(8,128)(2,1)S(1)} custom-call(bf16[4096,1024]{1,0:T(8,128)(2,1)S(1)} %get-tuple-element.22.held, f32[1,1024]{1,0:T(1,128)} %get-tuple-element.23.token), custom_call_target="tpu_custom_call" | custom-call | tf_op jit(solution)/shard_map/value/pallas_call | solution.py:525
  110.9 3.3 %write_value.1 = bf16[4096,1024]{1,0:T(8,128)(2,1)} custom-call(bf16[4096,1024]{1,0:T(8,128)(2,1)S(1)} %get-tuple-element.22.held, bf16[4096,1024]{1,0:T(8,128)(2,1)S(1)} %value.1), custom_call_target="tpu_custom_call" | custom-call | tf_op jit(solution)/shard_map/write_value/pallas_call | solution.py:539

commit v4 on v3

v4 whole, which is shorter than its diff:
```python
import functools
import math

import jax
import jax.numpy as jnp
from jax import lax
from jax.experimental import pallas as pl
from jax.experimental.pallas import tpu as pltpu
from jax.sharding import PartitionSpec as P

learn_rate = 0.2
hold_rate = 0.9
MESH = pl.DeviceIdType.MESH
UNITS = 8
PARTS = ((1, 2, 5), (8,), (2, 6))
HEAD_RUNS = (1, 1)
TAIL_RUNS = (2, 2, 1, 1)
SPLIT = 2
EARLY = 64
STEP = 32
START = 2
AHEAD = 3
PIECES = 32
VMEM_BYTES = 67_043_328


def plain(
    w_query,
    first_query,
    second_query,
    w_key,
    first_key,
    second_key,
    w_value,
    first_value,
    second_value,
    norm_gain,
    rows,
):
    gained = []
    for w, first, second in (
        (w_query, first_query, second_query),
        (w_key, first_key, second_key),
        (w_value, first_value, second_value),
    ):
        hold = hold_rate * first + second
        gained.append((w - learn_rate * hold) * norm_gain[:, None])
    totals = lax.psum(tuple(jnp.sum(jnp.abs(g), axis=0) for g in gained), "fsdp")
    factors = tuple(t / rows for t in totals)
    ready = tuple(
        lax.all_gather(
            (g / f).astype(jnp.bfloat16), "fsdp", axis=0, tiled=True
        )
        for g, f in zip(gained, factors)
    )
    return ready + factors


def units_of(cols):
    units = []
    for m, sizes in enumerate(PARTS):
        first = 0
        for size in sizes:
            units.append((m, first, size * cols // UNITS))
            first += size * cols // UNITS
    return units


def runs_of(sizes, cols, parts):
    runs = []
    first = 0
    for size in sizes:
        runs.append((first, size * cols // parts))
        first += size * cols // parts
    return runs


def places():
    me = lax.axis_index("fsdp")
    core = me % 2
    x = (me // 2) % 2
    y = me // 4
    partner = me + 1 - 2 * core
    x_near = me + 2 - 4 * x
    y_near = me + 4 - 8 * y
    diag = x_near + 4 - 8 * y
    return me, core, partner, x_near, y_near, diag


def block_of(ref, at, tall, c, width):
    return ref.at[pl.ds(pl.multiple_of(at, 16), tall), pl.ds(c, width)]


class Relay:
    def __init__(self, own, far, sems, send_sem):
        self.own, self.far, self.send_sem = own, far, send_sem
        self.x_recv, self.y_recv, self.rest, self.diag_recv = sems
        self.rows = far.shape[0] // 8
        self.half = self.rows // 2
        self.cols = far.shape[1]
        self.me, _, self.partner, self.x_near, self.y_near, self.diag = places()
        self.runs = runs_of(TAIL_RUNS, self.cols, sum(TAIL_RUNS))

    def send(self, source, at, tall, c, width, recv_sem, peer):
        pltpu.make_async_remote_copy(
            src_ref=block_of(source, at, tall, c, width),
            dst_ref=block_of(self.far, at, tall, c, width),
            send_sem=self.send_sem, recv_sem=recv_sem,
            device_id={"fsdp": peer}, device_id_type=MESH,
        ).start()

    def arrived(self, at, tall, c, width, recv_sem):
        ref = block_of(self.far, at, tall, c, width)
        pltpu.make_async_remote_copy(
            src_ref=ref, dst_ref=ref, send_sem=self.send_sem, recv_sem=recv_sem,
            device_id={"fsdp": self.partner}, device_id_type=MESH,
        ).wait_recv()

    def start(self):
        top = self.me * self.rows
        low = top + self.half
        for r, (c, width) in enumerate(self.runs):
            self.send(
                self.own, top, self.half, c, width, self.x_recv.at[r], self.x_near
            )
            self.send(
                self.own, low, self.half, c, width, self.y_recv.at[r], self.y_near
            )
        self.send(
            self.own, low, self.half, 0, self.cols, self.rest.at[0], self.x_near
        )
        self.send(
            self.own, top, self.half, 0, self.cols, self.rest.at[1], self.y_near
        )

    def take(self, r):
        c, width = self.runs[r]
        top = self.x_near * self.rows
        low = self.y_near * self.rows + self.half
        self.arrived(top, self.half, c, width, self.x_recv.at[r])
        self.arrived(low, self.half, c, width, self.y_recv.at[r])

    def forward(self, r, source):
        c, width = self.runs[r]
        top = self.x_near * self.rows
        low = self.y_near * self.rows + self.half
        self.send(
            source, top, self.half, c, width, self.diag_recv.at[0, r], self.y_near
        )
        self.send(
            source, low, self.half, c, width, self.diag_recv.at[1, r], self.x_near
        )

    def take_rest(self):
        for near, first, sem in (
            (self.x_near, self.half, self.rest.at[0]),
            (self.y_near, 0, self.rest.at[1]),
        ):
            self.arrived(near * self.rows + first, self.half, 0, self.cols, sem)

    def finish(self, r, then):
        c, width = self.runs[r]
        for h in range(2):
            at = self.diag * self.rows + h * self.half
            self.arrived(at, self.half, c, width, self.diag_recv.at[h, r])
            then(at, self.half, c, width)

    def left(self, blocks, c, width):
        ref = block_of(self.far, 0, blocks * self.rows, c, width)
        pltpu.make_async_remote_copy(
            src_ref=ref, dst_ref=ref, send_sem=self.send_sem,
            recv_sem=self.x_recv.at[0], device_id={"fsdp": self.partner},
            device_id_type=MESH,
        ).wait_send()


def gather_kernel(total_rows, *refs):
    ins, gain_ref = refs[:9], refs[9]
    outs, head, tail, factors = refs[10], refs[11], refs[12], refs[13:16]
    (
        bufs, gain_line, gain_buf, parts, early,
        load_sem, gain_sem, sum_send, sum_recv, early_send, early_recv,
        x_recv, y_recv, x_rest, y_rest, diag_recv,
        x_tail, y_tail, rest_tail, diag_tail, tail_send,
        chip_recv, chip_tail, send_sem, chip_send,
    ) = refs[16:]
    w_buf, first_buf, second_buf = (bufs.at[k] for k in range(3))
    rows, cols = bufs.shape[2:]
    half = rows // 2

    me, core, partner, x_near, y_near, diag = places()
    peers = [
        diag + 1 - 2 * core, diag, x_near + 1 - 2 * core, y_near + 1 - 2 * core,
        x_near, y_near, partner,
    ]
    units = units_of(cols)
    count = len(units)
    head_cols = head.shape[1]
    runs = runs_of(HEAD_RUNS, head_cols, sum(HEAD_RUNS))
    early_width = units[0][2]
    early_rows = half * early_width // cols
    head_rows = rows * head_cols // cols

    barrier = pltpu.get_barrier_semaphore()
    for peer in peers:
        pl.semaphore_signal(
            barrier, inc=1, device_id={"fsdp": peer}, device_id_type=MESH
        )

    def load(u):
        if u < count:
            m, c, width = units[u]
            at = pl.ds(c, width)
            for k in range(3):
                pltpu.make_async_copy(
                    ins[3 * m + k].at[:, at], bufs.at[k, m, :, at],
                    load_sem.at[u % 4],
                ).start()

    def loaded(u):
        m, c, width = units[u]
        ref = bufs.at[:, m, :, pl.ds(c, width)]
        pltpu.make_async_copy(ref, ref, load_sem.at[u % 4]).wait()

    gain_copy = pltpu.make_async_copy(gain_ref, gain_line, gain_sem)
    gain_copy.start()
    for u in range(START):
        load(u)

    gain_copy.wait()
    for k in range(rows // 128):
        line = gain_line[:, pl.ds(k * 128, 128)]
        gain_buf[pl.ds(k * 128, 128), :] = jnp.broadcast_to(line, (128, 128)).T

    def sums(u):
        m, c, width = units[u]
        loaded(u)
        if u == 0:
            for v in range(START, AHEAD):
                load(v)
        load(u + AHEAD)
        tiles = width // 128

        def body(i, acc):
            at = pl.ds(pl.multiple_of(i * STEP, STEP), STEP)
            gain = gain_buf[at, :]
            new = []
            for t in range(tiles):
                lanes = pl.ds(c + t * 128, 128)
                hold = hold_rate * first_buf[m, at, lanes] + second_buf[m, at, lanes]
                gained = (w_buf[m, at, lanes] - learn_rate * hold) * gain
                w_buf[m, at, lanes] = gained
                size = jnp.abs(gained)
                new.append(
                    acc[t] + jnp.sum(size.reshape(STEP // 8, 8, 128), axis=0)
                )
            return tuple(new)

        acc = lax.fori_loop(
            0, rows // STEP, body,
            tuple(jnp.zeros((8, 128), jnp.float32) for _ in range(tiles)),
        )
        for t in range(tiles):
            parts[me, m, :, pl.ds(c + t * 128, 128)] = jnp.sum(
                acc[t], axis=0, keepdims=True
            )

    def send_sums(u):
        m, c, width = units[u]
        at = pl.ds(c, width)
        ref = parts.at[me, m, :, at]
        for peer in peers:
            pltpu.make_async_remote_copy(
                src_ref=ref, dst_ref=ref, send_sem=sum_send,
                recv_sem=sum_recv.at[u],
                device_id={"fsdp": peer}, device_id_type=MESH,
            ).start()

    def block(m, owner, first, tall, c, width):
        at = owner * rows + first
        if m == 1:
            at = at + 8 * rows
        if m == 2:
            ref, c = (head, c) if c < head_cols else (tail, c - head_cols)
        else:
            ref = outs
        return block_of(ref, at, tall, c, width)

    def span(tall):
        return outs.at[pl.ds(0, tall), :]

    def send(ref, recv_sem, peer):
        pltpu.make_async_remote_copy(
            src_ref=ref, dst_ref=ref, send_sem=send_sem, recv_sem=recv_sem,
            device_id={"fsdp": peer}, device_id_type=MESH,
        ).start()

    def cross(ref, recv_sem):
        pltpu.make_async_remote_copy(
            src_ref=ref, dst_ref=ref, send_sem=chip_send, recv_sem=recv_sem,
            device_id={"fsdp": partner}, device_id_type=MESH,
        ).start()

    def arrived(ref, recv_sem):
        pltpu.make_async_remote_copy(
            src_ref=ref, dst_ref=ref, send_sem=send_sem, recv_sem=recv_sem,
            device_id={"fsdp": partner}, device_id_type=MESH,
        ).wait_recv()

    def left(ref, sem):
        pltpu.make_async_remote_copy(
            src_ref=ref, dst_ref=ref, send_sem=sem, recv_sem=chip_recv,
            device_id={"fsdp": partner}, device_id_type=MESH,
        ).wait_send()

    def early_copy(side, peer, first, tall):
        at = pl.ds(first, tall)
        return pltpu.make_async_remote_copy(
            src_ref=w_buf.at[0, at, pl.ds(0, early_width)],
            dst_ref=early.at[side, at], send_sem=early_send,
            recv_sem=early_recv.at[side],
            device_id={"fsdp": peer}, device_id_type=MESH,
        )

    def scaled(source, m, owner, lo, hi, c, width):
        scale = jnp.broadcast_to(
            1.0 / factors[m][:, pl.ds(c, width)], (16, width)
        )

        def body(i, carry):
            for k in range(STEP // 16):
                at = pl.multiple_of(i * STEP + k * 16, 16)
                tile = source[pl.ds(at, 16), pl.ds(c, width)] * scale
                block(m, owner, at, 16, c, width)[...] = tile.astype(jnp.bfloat16)
            return carry

        lax.fori_loop(lo // STEP, hi // STEP, body, 0)

    def finish(u):
        m, c, width = units[u]
        at = pl.ds(c, width)
        arrived(parts.at[pl.ds(0, 7), m, :, at], sum_recv.at[u])
        total = parts[0, m, :, at]
        for owner in range(1, 8):
            total = total + parts[owner, m, :, at]
        factors[m][:, at] = total / total_rows
        for h in (1, 0):
            scaled(w_buf.at[m], m, me, h * half, (h + 1) * half, c, width)
            if u == count - 1 or u == 0 and h == 0:
                continue
            ref = block(m, me, h * half, half, c, width)
            send(ref, x_recv.at[m] if h == 0 else x_rest, x_near)
            send(ref, y_recv.at[m] if h == 1 else y_rest, y_near)
        cross(
            block(m, me, 0, rows, c, width),
            chip_tail if u == count - 1 else chip_recv,
        )

    def take_early():
        for side, owner in enumerate((x_near, y_near)):
            arrived(early.at[side], early_recv.at[side])
            scaled(early.at[side], 0, owner, 0, half, 0, early_width)

    sums(0)
    pl.semaphore_wait(barrier, 7)
    send_sums(0)
    early_copy(0, x_near, 0, EARLY).start()
    early_copy(1, y_near, 0, EARLY).start()
    sums(1)
    send_sums(1)
    early_copy(0, x_near, EARLY, half - EARLY).start()
    early_copy(1, y_near, EARLY, half - EARLY).start()
    sums(2)
    send_sums(2)
    finish(0)
    finish(1)
    take_early()
    for u in range(3, count):
        sums(u)
        send_sums(u)
        finish(u - 1)
    finish(count - 1)

    widths = (cols, cols, head_cols)
    pieces = [
        (m, slot, c, width)
        for slot, (m, (c, width)) in enumerate(
            [(0, (0, cols)), (1, (0, cols))] + [(2, run) for run in runs]
        )
    ]
    for m in range(3):
        whole = half * widths[m] // cols
        arrived(span(whole - early_rows * (m == 0)), x_recv.at[m])
        arrived(span(whole), y_recv.at[m])
        for piece, slot, c, width in pieces:
            if piece == m:
                send(
                    block(m, x_near, 0, half, c, width), diag_recv.at[0, slot],
                    y_near,
                )
                send(
                    block(m, y_near, half, half, c, width), diag_recv.at[1, slot],
                    x_near,
                )

    relay = Relay(tail, tail, (x_tail, y_tail, rest_tail, diag_tail), tail_send)

    @pl.when(core == 0)
    def _():
        relay.start()

    arrived(span(2 * half + head_rows // 2), x_rest)
    arrived(span(2 * half + head_rows // 2 - early_rows), y_rest)
    for m in range(3):
        for owner in (x_near, y_near):
            cross(block(m, owner, 0, rows, 0, widths[m]), chip_recv)
    for m, slot, c, width in pieces:
        for h in range(2):
            ref = block(m, diag, h * half, half, c, width)
            arrived(ref, diag_recv.at[h, slot])
            cross(ref, chip_recv)

    @pl.when(core == 0)
    def _():
        for r in range(len(relay.runs)):
            relay.take(r)
            if r < SPLIT:
                relay.forward(r, tail)
        relay.take_rest()
        for r in range(SPLIT):
            relay.finish(r, lambda *at: None)
        relay.left(2, 0, relay.cols)
        relay.left(1, 0, relay.runs[SPLIT][0])

    arrived(span(4 * (2 * rows + head_rows)), chip_recv)
    arrived(tail.at[pl.ds(0, rows), :], chip_tail)
    left(span(3 * (2 * rows + head_rows) - 2 * early_rows), send_sem)
    left(span(4 * (2 * rows + head_rows) + rows - head_rows), chip_send)
    left(parts.at[pl.ds(0, 7)], sum_send)
    left(early, early_send)


def tail_kernel(held, token, value, *sems):
    *relay_sems, relay_send, chip_recv, chip_send, ready = sems
    rows = held.shape[0] // 8
    _, core, partner, x_near, y_near, diag = places()

    barrier = pltpu.get_barrier_semaphore()
    for peer in (x_near, y_near):
        pl.semaphore_signal(
            barrier, inc=1, device_id={"fsdp": peer}, device_id_type=MESH
        )

    @pl.when(core == 1)
    def _():
        pl.semaphore_signal(
            barrier, inc=1, device_id={"fsdp": partner}, device_id_type=MESH
        )

    pl.semaphore_wait(barrier, 3 - core)
    relay = Relay(held, value, relay_sems, relay_send)
    cols = relay.cols
    cut = relay.runs[SPLIT][0]

    def copy_of(source, at, tall, c, width):
        return pltpu.make_async_remote_copy(
            src_ref=block_of(source, at, tall, c, width),
            dst_ref=block_of(value, at, tall, c, width),
            send_sem=chip_send, recv_sem=chip_recv,
            device_id={"fsdp": partner}, device_id_type=MESH,
        )

    @pl.when(core == 0)
    def _():
        pl.semaphore_signal(
            ready, inc=1, device_id={"fsdp": partner}, device_id_type=MESH
        )
        for r in range(SPLIT, len(relay.runs)):
            relay.forward(r, held)
        for owner, width in ((x_near, cols), (y_near, cols), (diag, cut)):
            copy_of(held, owner * rows, rows, 0, width).start()
        for r in range(SPLIT, len(relay.runs)):
            relay.finish(r, lambda *at: copy_of(value, *at).start())
        relay.left(1, cut, cols - cut)

    @pl.when(core == 1)
    def _():
        relay.start()
        for r in range(len(relay.runs)):
            relay.take(r)
            relay.forward(r, value)
        relay.take_rest()
        pl.semaphore_wait(ready, 1)
        for owner in (x_near, y_near):
            copy_of(value, owner * rows, rows, 0, cols).start()
        for r in range(len(relay.runs)):
            relay.finish(r, lambda *at: copy_of(value, *at).start())
        relay.left(3, 0, cols)

    three = copy_of(value, 0, 3 * rows, 0, cols)
    three.wait_recv()
    three.wait_send()


def write_first(src, head, *refs):
    lines, outs, line_outs, sem = refs[:3], refs[3:6], refs[6:9], refs[9]
    copies = [
        pltpu.make_async_copy(lines[k], line_outs[k], sem.at[3 + k])
        for k in range(3)
    ]
    for copy in copies:
        copy.start()
    tall = outs[0].shape[0]
    step = tall // PIECES
    part = pl.ds(0, head.shape[1])
    for p in range(PIECES):
        at = pl.ds(p * step, step)
        for k in range(2):
            pltpu.make_async_copy(
                src.at[pl.ds(k * tall + p * step, step), :], outs[k].at[at, :],
                sem.at[k],
            ).start()
        pltpu.make_async_copy(
            head.at[at, :], outs[2].at[at, part], sem.at[2]
        ).start()
    for k in range(2):
        whole = src.at[pl.ds(k * tall, tall), :]
        pltpu.make_async_copy(whole, outs[k], sem.at[k]).wait()
    pltpu.make_async_copy(head, outs[2].at[:, part], sem.at[2]).wait()
    for copy in copies:
        copy.wait()


def write_last(held, value, first, out, sem):
    rows = out.shape[0] // 8
    width = held.shape[1]
    start = out.shape[1] - width
    cut = runs_of(TAIL_RUNS, width, sum(TAIL_RUNS))[SPLIT][0]
    me, core, _, x_near, y_near, diag = places()
    step = 8 * rows // PIECES

    def put(src, owner, c=0, wide=width):
        for p in range(rows // step):
            at = owner * rows + p * step
            pltpu.make_async_copy(
                block_of(src, at, step, c, wide),
                block_of(out, at, step, start + c, wide), sem,
            ).start()

    for k in range(2):
        put(held, me - core + k)
    for owner in (x_near, y_near, diag):
        put(value, owner + 1 - 2 * core)

    @pl.when(core == 0)
    def _():
        put(held, x_near)
        put(held, y_near)
        put(held, diag, 0, cut)
        put(value, diag, cut, width - cut)

    @pl.when(core == 1)
    def _():
        for owner in (x_near, y_near, diag):
            put(value, owner)

    whole = out.at[:, pl.ds(start, width)]
    pltpu.make_async_copy(value, whole, sem).wait()


def ringed(*args, total_rows):
    rows, cols = args[0].shape
    units = units_of(cols)
    count = len(units)
    vmem = pl.BlockSpec(memory_space=pltpu.VMEM)
    hbm = pl.BlockSpec(memory_space=pltpu.HBM)
    dma = pltpu.SemaphoreType.DMA
    tail_cols = units[-1][2]
    head = pltpu.VMEM((8 * rows, cols - tail_cols), jnp.bfloat16)
    tail = pltpu.VMEM((8 * rows, tail_cols), jnp.bfloat16)
    line = jax.ShapeDtypeStruct((1, cols), jnp.float32)
    runs = len(TAIL_RUNS)
    slots = 2 + len(HEAD_RUNS)
    relay = [dma((runs,)), dma((runs,)), dma((2,)), dma((2, runs)), dma]
    pair, head, held, *factors = pl.pallas_call(
        functools.partial(gather_kernel, total_rows),
        out_shape=[pltpu.VMEM((16 * rows, cols), jnp.bfloat16), head, tail]
        + [pltpu.VMEM((1, cols), jnp.float32)] * 3,
        in_specs=[hbm] * 10,
        out_specs=[vmem] * 6,
        scratch_shapes=[
            pltpu.VMEM((3, 3, rows, cols), jnp.float32),
            pltpu.VMEM((1, rows), jnp.float32),
            pltpu.VMEM((rows, 128), jnp.float32),
            pltpu.VMEM((8, 3, 1, cols), jnp.float32),
            pltpu.VMEM((2, rows // 2, units[0][2]), jnp.float32),
            dma((4,)), dma, dma, dma((count,)), dma, dma((2,)),
            dma((3,)), dma((3,)), dma, dma, dma((2, slots)),
            *relay, dma, dma, dma, dma,
        ],
        compiler_params=pltpu.CompilerParams(
            collective_id=0, has_side_effects=True,
            vmem_limit_bytes=VMEM_BYTES - 3 * 16 * rows * cols - 2**20,
        ),
        name="gather",
    )(*(
        pltpu.with_memory_space_constraint(a, pltpu.HBM)
        for a in (*args[:9], args[9].reshape(1, rows))
    ))
    ready = jax.ShapeDtypeStruct((8 * rows, cols), jnp.bfloat16)
    query, key, first, *lines = pl.pallas_call(
        write_first,
        out_shape=[ready] * 2 + [pltpu.HBM(ready.shape, ready.dtype)] + [line] * 3,
        in_specs=[vmem] * 5,
        out_specs=[hbm] * 6,
        scratch_shapes=[dma((6,))],
        compiler_params=pltpu.CompilerParams(
            has_side_effects=True, vmem_limit_bytes=2**20
        ),
        name="write_first",
    )(pair, head, *factors)
    value = pl.pallas_call(
        tail_kernel,
        out_shape=tail,
        in_specs=[vmem, hbm],
        out_specs=vmem,
        scratch_shapes=[*relay, dma, dma, pltpu.SemaphoreType.REGULAR],
        compiler_params=pltpu.CompilerParams(
            collective_id=1, has_side_effects=True, vmem_limit_bytes=2**20
        ),
        name="tail",
    )(held, pltpu.with_memory_space_constraint(lines[0], pltpu.HBM))
    value = pl.pallas_call(
        write_last,
        out_shape=pltpu.HBM(ready.shape, ready.dtype),
        in_specs=[vmem, vmem, hbm],
        out_specs=hbm,
        scratch_shapes=[dma],
        input_output_aliases={2: 0},
        compiler_params=pltpu.CompilerParams(vmem_limit_bytes=2**20),
        name="write_last",
    )(held, value, pltpu.with_memory_space_constraint(first, pltpu.HBM))
    return [query, key, value] + [f.reshape(cols) for f in lines]


def on_device(*args, devices):
    rows, cols = args[0].shape
    total_rows = devices * rows
    fits = rows * cols * (36 + 48) <= 48 * 2**20
    if devices == 8 and rows % 128 == 0 and cols % (128 * UNITS) == 0 and fits:
        return tuple(ringed(*args, total_rows=total_rows))
    return plain(*args, rows=total_rows)


def solution(mesh):
    return jax.shard_map(
        functools.partial(on_device, devices=mesh.shape["fsdp"]),
        mesh=mesh,
        in_specs=(P("fsdp", "model"),) * 9 + (P("fsdp"),),
        out_specs=(P(None, "model"),) * 3 + (P("model"),) * 3,
        check_vma=False,
    )
```

time: 114 us -> 114 us (level)
    pallas_call x3, Pallas kernels: 25.4 us -> 16.7 us  [the longest x1 7.66 us: ringed(): pl.pallas_call(tail_kernel, out_shape=tail, in_specs=[vmem, hbm], out_spe...]
    pallas_call x1, Pallas kernels: 88.1 us -> 96.1 us  [ringed(): pl.pallas_call(functools.partial(gather_kernel, total_rows), out_shape=[p...]
where the time goes in v4:
time: 114 us
  Pallas kernels  113 us (99%)
    pallas_call x1, Pallas kernels, ringed(): pl.pallas_call(functools.partial(gather_kernel, total_rows), out_shape=[p...  96.1 us
    pallas_call x1, Pallas kernels, ringed(): pl.pallas_call(tail_kernel, out_shape=tail, in_specs=[vmem, hbm], out_spe...  7.66 us
    pallas_call x1, Pallas kernels, ringed(): pl.pallas_call(write_first, out_shape=[ready] * 2 + [pltpu.HBM(ready.shap...  6.45 us
    pallas_call x1, Pallas kernels, ringed(): pl.pallas_call(write_last, out_shape=pltpu.HBM(ready.shape, ready.dtype),...  2.64 us

profile of v4, /device:TPU:0, one launch (start us, length us, event | category | flops | bytes accessed | tf_op | source)
XLA Modules:
  0.0 113.5 jit_solution(16646790811770692177)
XLA Ops:
  0.6 96.1 %gather.1 = (bf16[8192,1024]{1,0:T(8,128)(2,1)S(1)}, bf16[4096,256]{1,0:T(8,128)(2,1)S(1)}, bf16[4096,768]{1,0:T(8,128)(2,1)S(1)}, f32[1,1024]{1,0:T(1,128)S(1)}...) custom-call(f32[512,1024]{1,0:T(8,128)} %refs_0_.1, f32[512,1024]{1,0:T(8,128)} %refs_1_.1, f32[512,1024]{1,0:T(8,128)} %refs_2_.1, ...), custom_call_target="tpu_custom_call" | custom-call | tf_op jit(solution)/shard_map/gather/pallas_call | solution.py:585
  96.8 6.4 %write_first.1 = (bf16[4096,1024]{1,0:T(8,128)(2,1)}, bf16[4096,1024]{1,0:T(8,128)(2,1)}, bf16[4096,1024]{1,0:T(8,128)(2,1)}, f32[1,1024]{1,0:T(1,128)}, f32[1,1024]{1,0:T(1,128)}, /*index=5*/f32[1,1024]{1,0:T(1,128)}) custom-call(bf16[8192,1024]{1,0:T(8,128)(2,1)S(1)} %get-tuple-element.18.src, bf16[4096,256]{1,0:T(8,128)(2,1)S(1)} %get-tuple-element.19.head, ...), custom_call_target="tpu_custom_call" | custom-call | tf_op jit(solution)/shard_map/write_first/pallas_call | solution.py:611
  103.2 7.7 %tail.1.value = bf16[4096,768]{1,0:T(8,128)(2,1)S(1)} custom-call(bf16[4096,768]{1,0:T(8,128)(2,1)S(1)} %get-tuple-element.25.held, f32[1,1024]{1,0:T(1,128)} %get-tuple-element.26.token), custom_call_target="tpu_custom_call" | custom-call | tf_op jit(solution)/shard_map/tail/pallas_call | solution.py:622
  110.9 2.6 %write_last.1 = bf16[4096,1024]{1,0:T(8,128)(2,1)} custom-call(bf16[4096,768]{1,0:T(8,128)(2,1)S(1)} %get-tuple-element.25.held, bf16[4096,768]{1,0:T(8,128)(2,1)S(1)} %tail.1.value, bf16[4096,1024]{1,0:T(8,128)(2,1)} %get-tuple-element.27.first), custom_call_target="tpu_custom_call", output_to_operand_aliasing={{}: (2, {})} | custom-call | tf_op jit(solution)/shard_map/write_last/pallas_call | solution.py:633

commit v5 on v4

--- a/solution.py
+++ b/solution.py
@@ -15,11 +15,10 @@
 PARTS = ((1, 2, 5), (8,), (2, 6))
 HEAD_RUNS = (1, 1)
 TAIL_RUNS = (2, 2, 1, 1)
-SPLIT = 2
-EARLY = 64
+SPLIT = 3
+EARLY = 96
 STEP = 32
-START = 2
-AHEAD = 3
+AHEAD = 2
 PIECES = 32
 VMEM_BYTES = 67_043_328
 
@@ -214,20 +213,20 @@
             for k in range(3):
                 pltpu.make_async_copy(
                     ins[3 * m + k].at[:, at], bufs.at[k, m, :, at],
-                    load_sem.at[u % 4],
+                    load_sem.at[u % 2],
                 ).start()
 
     def loaded(u):
         m, c, width = units[u]
         ref = bufs.at[:, m, :, pl.ds(c, width)]
-        pltpu.make_async_copy(ref, ref, load_sem.at[u % 4]).wait()
+        pltpu.make_async_copy(ref, ref, load_sem.at[u % 2]).wait()
 
     gain_copy = pltpu.make_async_copy(gain_ref, gain_line, gain_sem)
     gain_copy.start()
-    for u in range(START):
-        load(u)
+    load(0)
 
     gain_copy.wait()
+    load(1)
     for k in range(rows // 128):
         line = gain_line[:, pl.ds(k * 128, 128)]
         gain_buf[pl.ds(k * 128, 128), :] = jnp.broadcast_to(line, (128, 128)).T
@@ -235,9 +234,6 @@
     def sums(u):
         m, c, width = units[u]
         loaded(u)
-        if u == 0:
-            for v in range(START, AHEAD):
-                load(v)
         load(u + AHEAD)
         tiles = width // 128
 
@@ -502,7 +498,7 @@
     three.wait_send()
 
 
-def write_first(src, head, *refs):
+def write_first(src, head, held, *refs):
     lines, outs, line_outs, sem = refs[:3], refs[3:6], refs[6:9], refs[9]
     copies = [
         pltpu.make_async_copy(lines[k], line_outs[k], sem.at[3 + k])
@@ -512,7 +508,10 @@
         copy.start()
     tall = outs[0].shape[0]
     step = tall // PIECES
-    part = pl.ds(0, head.shape[1])
+    width = head.shape[1]
+    part = pl.ds(0, width)
+    rows = tall // 8
+    me, core, *_ = places()
     for p in range(PIECES):
         at = pl.ds(p * step, step)
         for k in range(2):
@@ -523,9 +522,16 @@
         pltpu.make_async_copy(
             head.at[at, :], outs[2].at[at, part], sem.at[2]
         ).start()
+    own = pl.ds(pl.multiple_of((me - core) * rows, 16), 2 * rows)
+    rest = pl.ds(width, held.shape[1])
+    pair = pltpu.make_async_copy(
+        held.at[own, :], outs[2].at[own, rest], sem.at[6]
+    )
+    pair.start()
     for k in range(2):
         whole = src.at[pl.ds(k * tall, tall), :]
         pltpu.make_async_copy(whole, outs[k], sem.at[k]).wait()
+    pair.wait()
     pltpu.make_async_copy(head, outs[2].at[:, part], sem.at[2]).wait()
     for copy in copies:
         copy.wait()
@@ -536,7 +542,7 @@
     width = held.shape[1]
     start = out.shape[1] - width
     cut = runs_of(TAIL_RUNS, width, sum(TAIL_RUNS))[SPLIT][0]
-    me, core, _, x_near, y_near, diag = places()
+    _, core, _, x_near, y_near, diag = places()
     step = 8 * rows // PIECES
 
     def put(src, owner, c=0, wide=width):
@@ -547,8 +553,6 @@
                 block_of(out, at, step, start + c, wide), sem,
             ).start()
 
-    for k in range(2):
-        put(held, me - core + k)
     for owner in (x_near, y_near, diag):
         put(value, owner + 1 - 2 * core)
 
@@ -564,8 +568,9 @@
         for owner in (x_near, y_near, diag):
             put(value, owner)
 
-    whole = out.at[:, pl.ds(start, width)]
-    pltpu.make_async_copy(value, whole, sem).wait()
+    six = pl.ds(0, 6 * rows)
+    whole = out.at[six, pl.ds(start, width)]
+    pltpu.make_async_copy(value.at[six, :], whole, sem).wait()
 
 
 def ringed(*args, total_rows):
@@ -594,7 +599,7 @@
             pltpu.VMEM((rows, 128), jnp.float32),
             pltpu.VMEM((8, 3, 1, cols), jnp.float32),
             pltpu.VMEM((2, rows // 2, units[0][2]), jnp.float32),
-            dma((4,)), dma, dma, dma((count,)), dma, dma((2,)),
+            dma((2,)), dma, dma, dma((count,)), dma, dma((2,)),
             dma((3,)), dma((3,)), dma, dma, dma((2, slots)),
             *relay, dma, dma, dma, dma,
         ],
@@ -611,14 +616,14 @@
     query, key, first, *lines = pl.pallas_call(
         write_first,
         out_shape=[ready] * 2 + [pltpu.HBM(ready.shape, ready.dtype)] + [line] * 3,
-        in_specs=[vmem] * 5,
+        in_specs=[vmem] * 6,
         out_specs=[hbm] * 6,
-        scratch_shapes=[dma((6,))],
+        scratch_shapes=[dma((7,))],
         compiler_params=pltpu.CompilerParams(
             has_side_effects=True, vmem_limit_bytes=2**20
         ),
         name="write_first",
-    )(pair, head, *factors)
+    )(pair, head, held, *factors)
     value = pl.pallas_call(
         tail_kernel,
         out_shape=tail,

time: 114 us -> 113 us (level)
    pallas_call x1, Pallas kernels: 7.66 us -> 6.3 us  [ringed(): pl.pallas_call(tail_kernel, out_shape=tail, in_specs=[vmem, hbm], out_spe...]
where the time goes in v5:
time: 113 us
  Pallas kernels  112 us (99%)
    pallas_call x1, Pallas kernels, ringed(): pl.pallas_call(functools.partial(gather_kernel, total_rows), out_shape=[p...  96.7 us
    pallas_call x1, Pallas kernels, ringed(): pl.pallas_call(write_first, out_shape=[ready] * 2 + [pltpu.HBM(ready.shap...  6.99 us
    pallas_call x1, Pallas kernels, ringed(): pl.pallas_call(tail_kernel, out_shape=tail, in_specs=[vmem, hbm], out_spe...  6.3 us

profile of v5, /device:TPU:0, one launch (start us, length us, event | category | flops | bytes accessed | tf_op | source)
XLA Modules:
  0.0 112.8 jit_solution(3114365215809442960)
XLA Ops:
  0.6 96.7 %gather.1 = (bf16[8192,1024]{1,0:T(8,128)(2,1)S(1)}, bf16[4096,256]{1,0:T(8,128)(2,1)S(1)}, bf16[4096,768]{1,0:T(8,128)(2,1)S(1)}, f32[1,1024]{1,0:T(1,128)S(1)}...) custom-call(f32[512,1024]{1,0:T(8,128)} %refs_0_.1, f32[512,1024]{1,0:T(8,128)} %refs_1_.1, f32[512,1024]{1,0:T(8,128)} %refs_2_.1, ...), custom_call_target="tpu_custom_call" | custom-call | tf_op jit(solution)/shard_map/gather/pallas_call | solution.py:590
  97.3 7.0 %write_first.1 = (bf16[4096,1024]{1,0:T(8,128)(2,1)}, bf16[4096,1024]{1,0:T(8,128)(2,1)}, bf16[4096,1024]{1,0:T(8,128)(2,1)}, f32[1,1024]{1,0:T(1,128)}, f32[1,1024]{1,0:T(1,128)}, /*index=5*/f32[1,1024]{1,0:T(1,128)}) custom-call(bf16[8192,1024]{1,0:T(8,128)(2,1)S(1)} %get-tuple-element.18.src, bf16[4096,256]{1,0:T(8,128)(2,1)S(1)} %get-tuple-element.19.head, ...), custom_call_target="tpu_custom_call" | custom-call | tf_op jit(solution)/shard_map/write_first/pallas_call | solution.py:616
  104.3 6.3 %tail.1.value = bf16[4096,768]{1,0:T(8,128)(2,1)S(1)} custom-call(bf16[4096,768]{1,0:T(8,128)(2,1)S(1)} %get-tuple-element.20.held, f32[1,1024]{1,0:T(1,128)} %get-tuple-element.26.token), custom_call_target="tpu_custom_call" | custom-call | tf_op jit(solution)/shard_map/tail/pallas_call | solution.py:627
  110.6 2.2 %write_last.1 = bf16[4096,1024]{1,0:T(8,128)(2,1)} custom-call(bf16[4096,768]{1,0:T(8,128)(2,1)S(1)} %get-tuple-element.20.held, bf16[4096,768]{1,0:T(8,128)(2,1)S(1)} %tail.1.value, bf16[4096,1024]{1,0:T(8,128)(2,1)} %get-tuple-element.27.first), custom_call_target="tpu_custom_call", output_to_operand_aliasing={{}: (2, {})} | custom-call | tf_op jit(solution)/shard_map/write_last/pallas_call | solution.py:638

commit v6 on v5

--- a/solution.py
+++ b/solution.py
@@ -16,6 +16,7 @@
 HEAD_RUNS = (1, 1)
 TAIL_RUNS = (2, 2, 1, 1)
 SPLIT = 3
+DIRECT = 2
 EARLY = 96
 STEP = 32
 AHEAD = 2
@@ -177,8 +178,8 @@
     ins, gain_ref = refs[:9], refs[9]
     outs, head, tail, factors = refs[10], refs[11], refs[12], refs[13:16]
     (
-        bufs, gain_line, gain_buf, parts, early,
-        load_sem, gain_sem, sum_send, sum_recv, early_send, early_recv,
+        bufs, gain_line, gain_buf, parts, pair, early,
+        load_sem, gain_sem, sum_send, sum_recv, pair_recv, early_send, early_recv,
         x_recv, y_recv, x_rest, y_rest, diag_recv,
         x_tail, y_tail, rest_tail, diag_tail, tail_send,
         chip_recv, chip_tail, send_sem, chip_send,
@@ -265,7 +266,7 @@
         m, c, width = units[u]
         at = pl.ds(c, width)
         ref = parts.at[me, m, :, at]
-        for peer in peers:
+        for peer in peers if u < DIRECT else (diag, x_near, y_near):
             pltpu.make_async_remote_copy(
                 src_ref=ref, dst_ref=ref, send_sem=sum_send,
                 recv_sem=sum_recv.at[u],
@@ -335,10 +336,25 @@
     def finish(u):
         m, c, width = units[u]
         at = pl.ds(c, width)
-        arrived(parts.at[pl.ds(0, 7), m, :, at], sum_recv.at[u])
-        total = parts[0, m, :, at]
-        for owner in range(1, 8):
-            total = total + parts[owner, m, :, at]
+        if u < DIRECT:
+            arrived(parts.at[pl.ds(0, 7), m, :, at], sum_recv.at[u])
+            total = parts[0, m, :, at]
+            for owner in range(1, 8):
+                total = total + parts[owner, m, :, at]
+        else:
+            arrived(parts.at[pl.ds(0, 3), m, :, at], sum_recv.at[u])
+            total = parts[core, m, :, at]
+            for k in range(1, 4):
+                total = total + parts[core + 2 * k, m, :, at]
+            pair[core, m, :, at] = total
+            ref = pair.at[core, m, :, at]
+            pltpu.make_async_remote_copy(
+                src_ref=ref, dst_ref=ref, send_sem=sum_send,
+                recv_sem=pair_recv.at[u - DIRECT],
+                device_id={"fsdp": partner}, device_id_type=MESH,
+            ).start()
+            arrived(pair.at[0, m, :, at], pair_recv.at[u - DIRECT])
+            total = pair[0, m, :, at] + pair[1, m, :, at]
         factors[m][:, at] = total / total_rows
         for h in (1, 0):
             scaled(w_buf.at[m], m, me, h * half, (h + 1) * half, c, width)
@@ -371,11 +387,14 @@
     finish(0)
     finish(1)
     take_early()
-    for u in range(3, count):
+    sums(3)
+    send_sums(3)
+    finish(2)
+    for u in range(4, count):
         sums(u)
         send_sums(u)
-        finish(u - 1)
-    finish(count - 1)
+    for u in range(3, count):
+        finish(u)
 
     widths = (cols, cols, head_cols)
     pieces = [
@@ -432,7 +451,9 @@
     arrived(tail.at[pl.ds(0, rows), :], chip_tail)
     left(span(3 * (2 * rows + head_rows) - 2 * early_rows), send_sem)
     left(span(4 * (2 * rows + head_rows) + rows - head_rows), chip_send)
-    left(parts.at[pl.ds(0, 7)], sum_send)
+    direct = units[DIRECT][1]
+    sent = (7 * direct + 4 * (3 * cols - direct)) // 21
+    left(parts.at[pl.ds(0, 7), :, :, pl.ds(0, sent)], sum_send)
     left(early, early_send)
 
 
@@ -598,8 +619,9 @@
             pltpu.VMEM((1, rows), jnp.float32),
             pltpu.VMEM((rows, 128), jnp.float32),
             pltpu.VMEM((8, 3, 1, cols), jnp.float32),
+            pltpu.VMEM((2, 3, 1, cols), jnp.float32),
             pltpu.VMEM((2, rows // 2, units[0][2]), jnp.float32),
-            dma((2,)), dma, dma, dma((count,)), dma, dma((2,)),
+            dma((2,)), dma, dma, dma((count,)), dma((count - DIRECT,)), dma, dma((2,)),
             dma((3,)), dma((3,)), dma, dma, dma((2, slots)),
             *relay, dma, dma, dma, dma,
         ],

time: 113 us -> 113 us (level)
  no operation moved by 1% of the time
where the time goes in v6:
time: 113 us; the launch traced here: 112 us
  Pallas kernels  112 us (99%)
    pallas_call x1, Pallas kernels, ringed(): pl.pallas_call(functools.partial(gather_kernel, total_rows), out_shape=[p...  96.3 us
    pallas_call x1, Pallas kernels, ringed(): pl.pallas_call(write_first, out_shape=[ready] * 2 + [pltpu.HBM(ready.shap...  6.99 us
    pallas_call x1, Pallas kernels, ringed(): pl.pallas_call(tail_kernel, out_shape=tail, in_specs=[vmem, hbm], out_spe...  6.29 us

profile of v6, /device:TPU:0, one launch (start us, length us, event | category | flops | bytes accessed | tf_op | source)
XLA Modules:
  0.0 112.4 jit_solution(806762615234681838)
XLA Ops:
  0.6 96.3 %gather.1 = (bf16[8192,1024]{1,0:T(8,128)(2,1)S(1)}, bf16[4096,256]{1,0:T(8,128)(2,1)S(1)}, bf16[4096,768]{1,0:T(8,128)(2,1)S(1)}, f32[1,1024]{1,0:T(1,128)S(1)}...) custom-call(f32[512,1024]{1,0:T(8,128)} %refs_0_.1, f32[512,1024]{1,0:T(8,128)} %refs_1_.1, f32[512,1024]{1,0:T(8,128)} %refs_2_.1, ...), custom_call_target="tpu_custom_call" | custom-call | tf_op jit(solution)/shard_map/gather/pallas_call | solution.py:611
  96.9 7.0 %write_first.1 = (bf16[4096,1024]{1,0:T(8,128)(2,1)}, bf16[4096,1024]{1,0:T(8,128)(2,1)}, bf16[4096,1024]{1,0:T(8,128)(2,1)}, f32[1,1024]{1,0:T(1,128)}, f32[1,1024]{1,0:T(1,128)}, /*index=5*/f32[1,1024]{1,0:T(1,128)}) custom-call(bf16[8192,1024]{1,0:T(8,128)(2,1)S(1)} %get-tuple-element.18.src, bf16[4096,256]{1,0:T(8,128)(2,1)S(1)} %get-tuple-element.19.head, ...), custom_call_target="tpu_custom_call" | custom-call | tf_op jit(solution)/shard_map/write_first/pallas_call | solution.py:638
  103.9 6.3 %tail.1.value = bf16[4096,768]{1,0:T(8,128)(2,1)S(1)} custom-call(bf16[4096,768]{1,0:T(8,128)(2,1)S(1)} %get-tuple-element.20.held, f32[1,1024]{1,0:T(1,128)} %get-tuple-element.26.token), custom_call_target="tpu_custom_call" | custom-call | tf_op jit(solution)/shard_map/tail/pallas_call | solution.py:649
  110.2 2.2 %write_last.1 = bf16[4096,1024]{1,0:T(8,128)(2,1)} custom-call(bf16[4096,768]{1,0:T(8,128)(2,1)S(1)} %get-tuple-element.20.held, bf16[4096,768]{1,0:T(8,128)(2,1)S(1)} %tail.1.value, bf16[4096,1024]{1,0:T(8,128)(2,1)} %get-tuple-element.27.first), custom_call_target="tpu_custom_call", output_to_operand_aliasing={{}: (2, {})} | custom-call | tf_op jit(solution)/shard_map/write_last/pallas_call | solution.py:660

commit v7 on v6

--- a/solution.py
+++ b/solution.py
@@ -13,9 +13,8 @@
 MESH = pl.DeviceIdType.MESH
 UNITS = 8
 PARTS = ((1, 2, 5), (8,), (2, 6))
-HEAD_RUNS = (1, 1)
+HEAD_RUNS = (2,)
 TAIL_RUNS = (2, 2, 1, 1)
-SPLIT = 3
 DIRECT = 2
 EARLY = 96
 STEP = 32
@@ -439,13 +438,11 @@
     def _():
         for r in range(len(relay.runs)):
             relay.take(r)
-            if r < SPLIT:
-                relay.forward(r, tail)
+            relay.forward(r, tail)
         relay.take_rest()
-        for r in range(SPLIT):
+        for r in range(len(relay.runs)):
             relay.finish(r, lambda *at: None)
-        relay.left(2, 0, relay.cols)
-        relay.left(1, 0, relay.runs[SPLIT][0])
+        relay.left(3, 0, relay.cols)
 
     arrived(span(4 * (2 * rows + head_rows)), chip_recv)
     arrived(tail.at[pl.ds(0, rows), :], chip_tail)
@@ -463,21 +460,16 @@
     _, core, partner, x_near, y_near, diag = places()
 
     barrier = pltpu.get_barrier_semaphore()
-    for peer in (x_near, y_near):
-        pl.semaphore_signal(
-            barrier, inc=1, device_id={"fsdp": peer}, device_id_type=MESH
-        )
-
     @pl.when(core == 1)
     def _():
-        pl.semaphore_signal(
-            barrier, inc=1, device_id={"fsdp": partner}, device_id_type=MESH
-        )
-
-    pl.semaphore_wait(barrier, 3 - core)
+        for peer in (x_near, y_near, partner):
+            pl.semaphore_signal(
+                barrier, inc=1, device_id={"fsdp": peer}, device_id_type=MESH
+            )
+
+    pl.semaphore_wait(barrier, 1 + core)
     relay = Relay(held, value, relay_sems, relay_send)
     cols = relay.cols
-    cut = relay.runs[SPLIT][0]
 
     def copy_of(source, at, tall, c, width):
         return pltpu.make_async_remote_copy(
@@ -492,13 +484,8 @@
         pl.semaphore_signal(
             ready, inc=1, device_id={"fsdp": partner}, device_id_type=MESH
         )
-        for r in range(SPLIT, len(relay.runs)):
-            relay.forward(r, held)
-        for owner, width in ((x_near, cols), (y_near, cols), (diag, cut)):
-            copy_of(held, owner * rows, rows, 0, width).start()
-        for r in range(SPLIT, len(relay.runs)):
-            relay.finish(r, lambda *at: copy_of(value, *at).start())
-        relay.left(1, cut, cols - cut)
+        for owner in (x_near, y_near, diag):
+            copy_of(held, owner * rows, rows, 0, cols).start()
 
     @pl.when(core == 1)
     def _():
@@ -562,16 +549,15 @@
     rows = out.shape[0] // 8
     width = held.shape[1]
     start = out.shape[1] - width
-    cut = runs_of(TAIL_RUNS, width, sum(TAIL_RUNS))[SPLIT][0]
     _, core, _, x_near, y_near, diag = places()
     step = 8 * rows // PIECES
 
-    def put(src, owner, c=0, wide=width):
+    def put(src, owner):
         for p in range(rows // step):
             at = owner * rows + p * step
             pltpu.make_async_copy(
-                block_of(src, at, step, c, wide),
-                block_of(out, at, step, start + c, wide), sem,
+                block_of(src, at, step, 0, width),
+                block_of(out, at, step, start, width), sem,
             ).start()
 
     for owner in (x_near, y_near, diag):
@@ -579,10 +565,8 @@
 
     @pl.when(core == 0)
     def _():
-        put(held, x_near)
-        put(held, y_near)
-        put(held, diag, 0, cut)
-        put(value, diag, cut, width - cut)
+        for owner in (x_near, y_near, diag):
+            put(held, owner)
 
     @pl.when(core == 1)
     def _():

time: 113 us -> 113 us (level)
    pallas_call x1, Pallas kernels: 6.29 us -> 5.05 us  [ringed(): pl.pallas_call(tail_kernel, out_shape=tail, in_specs=[vmem, hbm], out_spe...]
    pallas_call x1, Pallas kernels: 96.3 us -> 97.5 us  [ringed(): pl.pallas_call(functools.partial(gather_kernel, total_rows), out_shape=[p...]
where the time goes in v7:
time: 113 us; the launch traced here: 112 us
  Pallas kernels  112 us (99%)
    pallas_call x1, Pallas kernels, ringed(): pl.pallas_call(functools.partial(gather_kernel, total_rows), out_shape=[p...  97.5 us
    pallas_call x1, Pallas kernels, ringed(): pl.pallas_call(write_first, out_shape=[ready] * 2 + [pltpu.HBM(ready.shap...  6.99 us
    pallas_call x1, Pallas kernels, ringed(): pl.pallas_call(tail_kernel, out_shape=tail, in_specs=[vmem, hbm], out_spe...  5.05 us

profile of v7, /device:TPU:0, one launch (start us, length us, event | category | flops | bytes accessed | tf_op | source)
XLA Modules:
  0.0 112.4 jit_solution(4382772233435615302)
XLA Ops:
  0.6 97.5 %gather.1 = (bf16[8192,1024]{1,0:T(8,128)(2,1)S(1)}, bf16[4096,256]{1,0:T(8,128)(2,1)S(1)}, bf16[4096,768]{1,0:T(8,128)(2,1)S(1)}, f32[1,1024]{1,0:T(1,128)S(1)}...) custom-call(f32[512,1024]{1,0:T(8,128)} %refs_0_.1, f32[512,1024]{1,0:T(8,128)} %refs_1_.1, f32[512,1024]{1,0:T(8,128)} %refs_2_.1, ...), custom_call_target="tpu_custom_call" | custom-call | tf_op jit(solution)/shard_map/gather/pallas_call | solution.py:595
  98.1 7.0 %write_first.1 = (bf16[4096,1024]{1,0:T(8,128)(2,1)}, bf16[4096,1024]{1,0:T(8,128)(2,1)}, bf16[4096,1024]{1,0:T(8,128)(2,1)}, f32[1,1024]{1,0:T(1,128)}, f32[1,1024]{1,0:T(1,128)}, /*index=5*/f32[1,1024]{1,0:T(1,128)}) custom-call(bf16[8192,1024]{1,0:T(8,128)(2,1)S(1)} %get-tuple-element.18.src, bf16[4096,256]{1,0:T(8,128)(2,1)S(1)} %get-tuple-element.19.head, ...), custom_call_target="tpu_custom_call" | custom-call | tf_op jit(solution)/shard_map/write_first/pallas_call | solution.py:622
  105.1 5.0 %tail.1.value = bf16[4096,768]{1,0:T(8,128)(2,1)S(1)} custom-call(bf16[4096,768]{1,0:T(8,128)(2,1)S(1)} %get-tuple-element.20.held, f32[1,1024]{1,0:T(1,128)} %get-tuple-element.26.token), custom_call_target="tpu_custom_call" | custom-call | tf_op jit(solution)/shard_map/tail/pallas_call | solution.py:633
  110.2 2.2 %write_last.1 = bf16[4096,1024]{1,0:T(8,128)(2,1)} custom-call(bf16[4096,768]{1,0:T(8,128)(2,1)S(1)} %get-tuple-element.20.held, bf16[4096,768]{1,0:T(8,128)(2,1)S(1)} %tail.1.value, bf16[4096,1024]{1,0:T(8,128)(2,1)} %get-tuple-element.27.first), custom_call_target="tpu_custom_call", output_to_operand_aliasing={{}: (2, {})} | custom-call | tf_op jit(solution)/shard_map/write_last/pallas_call | solution.py:644
